TPU v7x, 256 devices: a whole 4x4x8 slice. The times are simulated.
256 devices in a mesh: pitch: 8 (over x, core), span: 32 (over z, y).
Axes of the slice: x: 4, y: 4, z: 8, core: 2. Of those that a mesh axis runs over, the one named last changes fastest.
Arguments:
- residual: float32 [5, 4, 256, 1024], P(None, None, 'span', 'pitch'), may hold values from -0.6 to 0.6
- inverse_diagonal: float32 [5, 5, 4, 256, 1024], P(None, None, None, 'span', 'pitch'), may hold values from -0.1 to 1, as said below
- prior_increment: float32 [5, 4, 256, 1024], P(None, None, 'span', 'pitch'), may hold values from -3 to 3
- coupling: float32 [6, 5, 5], replicated, may hold values from -1 to 1
- characteristic: float32 [2, 2, 512, 5, 5], replicated, may hold values from -6 to 6
- cutoffs: int32 [2], replicated, may hold values from 128 to 512
Outputs:
- update: float32 [5, 4, 256, 1024], P(None, None, 'span', 'pitch')
Inputs may be any that keep to these rules, and one draw needn't show every extreme that they name: `inverse_diagonal`: each cell's block is dominated by its diagonal; the sweeps' recurrences are stable.
All inputs are finite; a program needn't handle non-finite values.
Results may differ from a plain program's by a relative error of at most 0.0003.
Values sent between devices are 32-bit elements; how exact they have to be, the bound alone decides.
A program may use at most 64 MiB of HBM per device.

v0:
```python
import jax
import jax.numpy as jnp
from jax import lax
from jax.sharding import Mesh
from jax.sharding import PartitionSpec as P

NP = 1024
HARMONICS = 512
SPAN = ("span_0", "span_1")


highest = lax.Precision.HIGHEST


def extended(array, sides, width):
    for axis, dim in sides:
        size, length = (lax.axis_size(axis), array.shape[dim])
        up = [(i, (i + 1) % size) for i in range(size)]
        down = [(j, i) for i, j in up]
        last = lax.slice_in_dim(array, length - width, length, axis=dim)
        initial = lax.slice_in_dim(array, 0, width, axis=dim)
        before = lax.ppermute(last, axis, up)
        after = lax.ppermute(initial, axis, down)
        array = jnp.concatenate([before, array, after], axis=dim)
    return array


def nothing_yet(array, identity):
    return jax.tree.map(
        lambda part, zero: jnp.zeros_like(part) + jnp.asarray(zero, part.dtype), array, identity
    )


def collected_together(array, axis):
    leaves = jax.tree.leaves(array)
    turns = sorted(range(len(leaves)), key=lambda k: -leaves[k].size)
    width = (1, *leaves[turns[0]].shape)[-1]
    lines = [
        jnp.pad(leaves[k].reshape(-1), (0, -leaves[k].size % width)).reshape(-1, width)
        for k in turns
    ]
    both, at, found = (lax.all_gather(jnp.concatenate(lines), axis), 0, {})
    for k, line in zip(turns, lines):
        piece = both[:, at : at + len(line)].reshape(len(both), -1)
        found[k] = piece[:, : leaves[k].size].reshape(-1, *leaves[k].shape)
        at += len(line)
    numbers = iter(range(len(leaves)))
    return jax.tree.map(lambda _: found[next(numbers)], array)


def entering(array, axes, combine, identity, reverse):
    before = start = nothing_yet(array, identity)
    total = array
    for axis in reversed(axes):
        length, mine = (lax.axis_size(axis), lax.axis_index(axis))
        pieces = collected_together(total, axis)
        inside, total = (start, start)
        for k in reversed(range(length)) if reverse else range(length):
            passed = k > mine if reverse else k < mine
            total = combine(total, jax.tree.map(lambda part: part[k], pieces))
            inside = jax.tree.map(lambda new, old: jnp.where(passed, new, old), total, inside)
        before = combine(inside, before)
    return before


def angle_tables(pitch_index, harmonic_index, points):
    product = pitch_index[:, None] * harmonic_index[None, :] % points
    angles = product.astype(jnp.float32) * (2.0 * jnp.pi / points)
    return (jnp.cos(angles), jnp.sin(angles))


def forward_dft(spanwise_slices, cosine, sine):
    flat = spanwise_slices.reshape(-1, spanwise_slices.shape[-1])
    shape = spanwise_slices.shape[:-1] + (cosine.shape[1],)
    real_part = jnp.dot(flat, cosine, precision=highest).reshape(shape)
    imag_part = -jnp.dot(flat, sine, precision=highest).reshape(shape)
    return (real_part, imag_part)


def contract(matrix, spectrum):
    return jnp.einsum("pkij,pjrk->pirk", matrix, spectrum, precision=highest)


def apply_harmonics(real_part, imag_part, characteristic, cutoffs, points):
    char_real = characteristic[:, 0]
    char_imag = characteristic[:, 1]
    result_real_component = contract(char_real, real_part) - contract(char_imag, imag_part)
    out_imag = contract(char_real, imag_part) + contract(char_imag, real_part)
    harmonic = jnp.arange(real_part.shape[-1], dtype=jnp.int32)
    kept = (harmonic[None, :] < cutoffs[:, None]).astype(jnp.float32)
    weight = jnp.where(harmonic == 0, 1.0, 2.0).astype(jnp.float32) / points
    factor = (kept * weight[None, :])[:, None, None, :]
    return (result_real_component * factor, out_imag * factor)


def inverse_dft(result_real_component, out_imag, cosine, sine):
    shape = result_real_component.shape[:-1] + (cosine.shape[0],)
    flat_real = result_real_component.reshape(-1, result_real_component.shape[-1])
    flat_imag = out_imag.reshape(-1, out_imag.shape[-1])
    result = jnp.dot(flat_real, cosine.T, precision=highest) - jnp.dot(
        flat_imag, sine.T, precision=highest
    )
    return result.reshape(shape)


def mix_field(matrix, field):
    return jnp.einsum("ij,jarp->iarp", matrix, field, precision=highest)


def mix_vector(matrix, vector):
    return jnp.einsum("ij,jap->iap", matrix, vector, precision=highest)


def apply_block(block, vector):
    return jnp.einsum("ijap,jap->iap", block, vector, precision=highest)


def chain_maps(earlier, later):
    early_maps, early_offset = earlier
    trailing_maps, late_offset = later
    maps = jnp.einsum("ijap,jkap->ikap", trailing_maps, early_maps, precision=highest)
    return (maps, apply_block(trailing_maps, early_offset) + late_offset)


def local_maps(inverse_diagonal, sources, matrix, descending):
    variables = inverse_diagonal.shape[0]
    axial_cell_count = inverse_diagonal.shape[2]
    radial = inverse_diagonal.shape[3]
    pitch_cells = inverse_diagonal.shape[4]
    identity = jnp.broadcast_to(
        jnp.eye(variables, dtype=jnp.float32)[:, :, None, None],
        (variables, variables, axial_cell_count, pitch_cells),
    )
    zero_vector = jnp.zeros((variables, axial_cell_count, pitch_cells), jnp.float32)

    def compose(step_index, carry):
        maps, offset = carry
        row_index = radial - 1 - step_index if descending else step_index
        block = lax.dynamic_index_in_dim(inverse_diagonal, row_index, 3, keepdims=False)
        rhs_row = lax.dynamic_index_in_dim(sources, row_index, 2, keepdims=False)
        factor = -jnp.einsum("ijap,jk->ikap", block, matrix, precision=highest)
        inject = rhs_row if descending else apply_block(block, rhs_row)
        maps = jnp.einsum("ijap,jkap->ikap", factor, maps, precision=highest)
        return (maps, apply_block(factor, offset) + inject)

    return (lax.fori_loop(0, radial, compose, (identity, zero_vector)), (identity, zero_vector))


def sweep_rows(inverse_diagonal, sources, matrix, incoming, descending):
    radial = inverse_diagonal.shape[3]

    def advance(step_index, carry):
        previous, buffer = carry
        row_index = radial - 1 - step_index if descending else step_index
        block = lax.dynamic_index_in_dim(inverse_diagonal, row_index, 3, keepdims=False)
        rhs_row = lax.dynamic_index_in_dim(sources, row_index, 2, keepdims=False)
        if descending:
            current = rhs_row - apply_block(block, mix_vector(matrix, previous))
        else:
            current = apply_block(block, rhs_row - mix_vector(matrix, previous))
        buffer = lax.dynamic_update_index_in_dim(buffer, current, row_index, 2)
        return (current, buffer)

    _, result = lax.fori_loop(0, radial, advance, (incoming, jnp.zeros_like(sources)))
    return result


def body(residual, inverse_diagonal, prior_increment, coupling, characteristic, cutoffs):
    spanwise_slices = jnp.stack([residual[:, 0], residual[:, -1]])
    harmonic_index = jnp.arange(HARMONICS, dtype=jnp.int32)
    whole_lines = lax.all_to_all(spanwise_slices, "pitch", split_axis=2, concat_axis=3, tiled=True)
    cosine, sine = angle_tables(jnp.arange(NP, dtype=jnp.int32), harmonic_index, NP)
    real_part, imag_part = forward_dft(whole_lines, cosine, sine)
    result_real_component, out_imag = apply_harmonics(
        real_part, imag_part, characteristic, cutoffs, NP
    )
    line_correction = inverse_dft(result_real_component, out_imag, cosine, sine)
    correction = lax.all_to_all(line_correction, "pitch", split_axis=3, concat_axis=2, tiled=True)
    corrected = residual.at[:, 0].add(correction[0]).at[:, -1].add(correction[1])
    padded = extended(prior_increment, (("pitch", 3),), 1)
    axial_pad = jnp.pad(prior_increment, ((0, 0), (1, 1), (0, 0), (0, 0)))
    source = (
        corrected
        - mix_field(coupling[2], padded[..., :-2])
        - mix_field(coupling[3], padded[..., 2:])
    )
    source = (
        source
        - mix_field(coupling[4], axial_pad[:, :-2])
        - mix_field(coupling[5], axial_pad[:, 2:])
    )
    (forward_maps, forward_offset), identity_pair = local_maps(
        inverse_diagonal, source, coupling[0], False
    )
    forward_prefix = entering(
        (forward_maps, forward_offset), SPAN, chain_maps, identity_pair, False
    )
    forward_in = forward_prefix[1]
    star = sweep_rows(inverse_diagonal, source, coupling[0], forward_in, False)
    (backward_maps, backward_offset), identity_pair = local_maps(
        inverse_diagonal, star, coupling[1], True
    )
    backward_prefix = entering(
        (backward_maps, backward_offset), SPAN, chain_maps, identity_pair, True
    )
    backward_in = backward_prefix[1]
    return sweep_rows(inverse_diagonal, star, coupling[1], backward_in, True)


def solution(mesh):
    split = Mesh(mesh.devices.reshape(mesh.shape["pitch"], 8, 4), ("pitch", "span_0", "span_1"))
    placed = (
        P(None, None, SPAN, "pitch"),
        P(None, None, None, SPAN, "pitch"),
        P(None, None, SPAN, "pitch"),
        P(),
        P(),
        P(),
    )
    return jax.shard_map(
        body, mesh=split, in_specs=placed, out_specs=P(None, None, SPAN, "pitch"), check_vma=False
    )
```

profile of v0, /device:TPU:2, one launch (start us, length us, event | category | flops | bytes accessed | tf_op | source)
XLA Modules:
  0.0 421.1 jit_solution(502148207685383890)
XLA Ops:
  1.7 5.5 %all-to-all-start = ((f32[2,5,8,128]{3,0,1,2:T(2,128)}), f32[2,5,8,128]{3,0,1,2:T(2,128)S(1)}, u32[]{:S(2)}, u32[]{:S(2)}) async-start(f32[2,5,8,128]{3,0,1,2:T(2,128)} %copy.183), calls=%async_computation | async-start | bytes 81920 | tf_op jit(solution)/shard_map/all_to_all | solution.py:171
  12.5 9.0 %fusion.60 = f32[2,512,5]{1,2,0:T(8,128)S(1)} fusion(f32[2,5,1024]{2,1,0:T(8,128)S(1)} %reshape.403), kind=kOutput, calls=%fused_computation.87 | convolution fusion | flops 70254592 | bytes 61440 | tf_op jit(solution)/shard_map/dot_general | solution.py:75
  21.5 9.0 %fusion.66 = f32[2,512,5]{1,2,0:T(8,128)S(1)} fusion(f32[2,5,1024]{2,1,0:T(8,128)S(1)} %reshape.403), kind=kOutput, calls=%fused_computation.89 | convolution fusion | flops 70259712 | bytes 61440 | tf_op jit(solution)/shard_map/dot_general | solution.py:76
  30.8 10.3 %fusion.71 = f32[10,1024]{1,0:T(8,128)S(1)} fusion(f32[10,512]{1,0:T(8,128)S(1)} %reshape.302), kind=kOutput, calls=%fused_computation.92 | convolution fusion | flops 70254592 | bytes 61440 | tf_op jit(solution)/shard_map/dot_general | solution.py:100
  41.1 20.6 %convolution_subtract_fusion.1 = f32[10,1024]{1,0:T(8,128)S(1)} fusion(f32[10,1024]{1,0:T(8,128)S(1)} %fusion.71, f32[10,512]{1,0:T(8,128)S(1)} %reshape.303), kind=kOutput, calls=%fused_computation.86 | convolution fusion | flops 70264832 | bytes 102400 | tf_op jit(solution)/shard_map/dot_general | solution.py:100
  64.4 6.7 %all-to-all-start.1 = ((f32[8,1,1280]{2,1,0:T(1,128)}), f32[8,1,1280]{2,1,0:T(1,128)S(1)}, u32[]{:S(2)}, u32[]{:S(2)}) async-start(f32[8,1,1280]{2,1,0:T(1,128)} %reshape.404), calls=%async_computation.1 | async-start | bytes 81920 | tf_op jit(solution)/shard_map/all_to_all | solution.py:178
  82.8 85.9 %while.67 = (s32[]{:T(128)}, f32[5,5,4,128]{1,0,3,2:T(8,128)}, f32[5,4,128]{0,2,1:T(8,128)S(1)}, f32[5,5,4,8,128]{4,1,2,0,3:T(8,128)S(1)}, f32[5,5]{0,1:T(8,128)S(1)}, /*index=5*/f32[5,4,8,128]{3,2,1,0:T(8,128)}, s32[]{:T(128)}) while((s32[]{:T(128)}, f32[5,5,4,128]{1,0,3,2:T(8,128)}, f32[5,4,128]{0,2,1:T(8,128)S(1)}, ...), condition=%wide.region_1.2_spmd, body=%wide.region_0.1_spmd.sunk | while | flops 1728002 | bytes 936053 | solution.py:146
  88.7 4.9 %convolution_bitcast_fusion.10 = f32[5,5,4,128]{1,0,3,2:T(8,128)} fusion(f32[5,5,4,128]{1,0,3,2:T(8,128)S(1)} %copy.596, f32[5,5,4,128]{1,0,3,2:T(8,128)S(1)} %copy.648), kind=kOutput, calls=%fused_computation.clone.1 | convolution fusion | flops 768000 | bytes 153600 | tf_op jit(solution)/shard_map/while/body/eval_jaxpr/ijap,jkap->ikap/dot_general | solution.py:143
  99.4 4.9 %convolution_bitcast_fusion.10 = f32[5,5,4,128]{1,0,3,2:T(8,128)} fusion(f32[5,5,4,128]{1,0,3,2:T(8,128)S(1)} %copy.596, f32[5,5,4,128]{1,0,3,2:T(8,128)S(1)} %copy.648), kind=kOutput, calls=%fused_computation.clone.1 | convolution fusion | flops 768000 | bytes 153600 | tf_op jit(solution)/shard_map/while/body/eval_jaxpr/ijap,jkap->ikap/dot_general | solution.py:143
  110.1 4.9 %convolution_bitcast_fusion.10 = f32[5,5,4,128]{1,0,3,2:T(8,128)} fusion(f32[5,5,4,128]{1,0,3,2:T(8,128)S(1)} %copy.596, f32[5,5,4,128]{1,0,3,2:T(8,128)S(1)} %copy.648), kind=kOutput, calls=%fused_computation.clone.1 | convolution fusion | flops 768000 | bytes 153600 | tf_op jit(solution)/shard_map/while/body/eval_jaxpr/ijap,jkap->ikap/dot_general | solution.py:143
  120.9 4.9 %convolution_bitcast_fusion.10 = f32[5,5,4,128]{1,0,3,2:T(8,128)} fusion(f32[5,5,4,128]{1,0,3,2:T(8,128)S(1)} %copy.596, f32[5,5,4,128]{1,0,3,2:T(8,128)S(1)} %copy.648), kind=kOutput, calls=%fused_computation.clone.1 | convolution fusion | flops 768000 | bytes 153600 | tf_op jit(solution)/shard_map/while/body/eval_jaxpr/ijap,jkap->ikap/dot_general | solution.py:143
  131.6 4.9 %convolution_bitcast_fusion.10 = f32[5,5,4,128]{1,0,3,2:T(8,128)} fusion(f32[5,5,4,128]{1,0,3,2:T(8,128)S(1)} %copy.596, f32[5,5,4,128]{1,0,3,2:T(8,128)S(1)} %copy.648), kind=kOutput, calls=%fused_computation.clone.1 | convolution fusion | flops 768000 | bytes 153600 | tf_op jit(solution)/shard_map/while/body/eval_jaxpr/ijap,jkap->ikap/dot_general | solution.py:143
  142.3 4.9 %convolution_bitcast_fusion.10 = f32[5,5,4,128]{1,0,3,2:T(8,128)} fusion(f32[5,5,4,128]{1,0,3,2:T(8,128)S(1)} %copy.596, f32[5,5,4,128]{1,0,3,2:T(8,128)S(1)} %copy.648), kind=kOutput, calls=%fused_computation.clone.1 | convolution fusion | flops 768000 | bytes 153600 | tf_op jit(solution)/shard_map/while/body/eval_jaxpr/ijap,jkap->ikap/dot_general | solution.py:143
  153.1 4.9 %convolution_bitcast_fusion.10 = f32[5,5,4,128]{1,0,3,2:T(8,128)} fusion(f32[5,5,4,128]{1,0,3,2:T(8,128)S(1)} %copy.596, f32[5,5,4,128]{1,0,3,2:T(8,128)S(1)} %copy.648), kind=kOutput, calls=%fused_computation.clone.1 | convolution fusion | flops 768000 | bytes 153600 | tf_op jit(solution)/shard_map/while/body/eval_jaxpr/ijap,jkap->ikap/dot_general | solution.py:143
  163.8 4.9 %convolution_bitcast_fusion.10 = f32[5,5,4,128]{1,0,3,2:T(8,128)} fusion(f32[5,5,4,128]{1,0,3,2:T(8,128)S(1)} %copy.596, f32[5,5,4,128]{1,0,3,2:T(8,128)S(1)} %copy.648), kind=kOutput, calls=%fused_computation.clone.1 | convolution fusion | flops 768000 | bytes 153600 | tf_op jit(solution)/shard_map/while/body/eval_jaxpr/ijap,jkap->ikap/dot_general | solution.py:143
  170.9 12.6 %all-gather = f32[480,128]{1,0:T(8,128)S(1)} all-gather(f32[120,128]{1,0:T(8,128)S(1)} %pad_maximum_fusion.5), channel_id=2, replica_groups=mesh['pitch'=8,'span_0'=8,'span_1'=4] {'span_1'}, dimensions={0}, use_global_device_ids=true | all-gather | bytes 307200 | tf_op jit(solution)/shard_map/all_gather | solution.py:42
  192.3 5.1 %fusion.79 = f32[4,128,5,5]{3,2,1,0:T(8,128)S(1)} fusion(f32[5,5,4,128]{1,0,3,2:T(8,128)} %copy.211, f32[5,5]{0,1:T(8,128)S(1)} %fusion.105), kind=kOutput, calls=%fused_computation.96 | convolution fusion | flops 768000 | bytes 102500 | tf_op jit(solution)/shard_map/ijap,jkap->ikap/dot_general | solution.py:121
  213.5 28.6 %all-gather.1 = f32[960,128]{1,0:T(8,128)S(1)} all-gather(f32[120,128]{1,0:T(8,128)S(1)} %pad_maximum_fusion.6), channel_id=3, replica_groups=mesh['pitch'=8,'span_0'=8,'span_1'=4] {'span_0'}, dimensions={0}, use_global_device_ids=true | all-gather | bytes 552960 | tf_op jit(solution)/shard_map/all_gather | solution.py:42
  252.6 6.2 %multiply_reduce_fusion.3 = f32[4,128,5]{2,1,0:T(8,128)S(1)} fusion(f32[5,5,4,128]{0,1,3,2:T(8,128)} %fusion.46, f32[4,128,5,5]{3,2,1,0:T(8,128)} %copy-done.3, f32[4,128,5,5]{3,2,1,0:T(8,128)} %copy-done.1, f32[4,128,5,5]{3,2,1,0:T(8,128)S(1)} %fusion.79, f32[4,128,5]{2,1,0:T(8,128)S(1)} %copy.532, f32[5,5]{0,1:T(8,128)S(1)} %fusion.105, pred[]{:T(512)S(6)} %gt.47, ...), kind=kOutput, calls=%fused_computation.72 | convolution fusion | flops 842240 | bytes 225384 | tf_op jit(solution)/shard_map/ijap,jkap->ikap/dot_general | solution.py:121
  260.0 10.4 %while.68 = (s32[]{:T(128)}, f32[5,4,128]{2,1,0:T(4,128)S(1)}, f32[5,4,8,128]{3,2,1,0:T(8,128)S(1)}, f32[5,4,8,128]{3,0,2,1:T(8,128)S(1)}, f32[5,5]{1,0:T(8,128)...) while((s32[]{:T(128)}, f32[5,4,128]{2,1,0:T(4,128)S(1)}, f32[5,4,8,128]{3,2,1,0:T(8,128)S(1)}, ...), condition=%wide.region_3.4_spmd, body=%wide.region_2.3_spmd.sunk | while | flops 179202 | bytes 245957 | solution.py:164
  271.9 60.0 %while.70 = (s32[]{:T(128)}, f32[5,5,4,128]{1,0,3,2:T(8,128)}, f32[5,4,128]{2,1,0:T(4,128)S(1)}, f32[5,5,4,8,128]{4,1,2,0,3:T(8,128)S(1)}, f32[5,5]{0,1:T(8,128)...) while((s32[]{:T(128)}, f32[5,5,4,128]{1,0,3,2:T(8,128)}, ...), condition=%wide.region_5.6_spmd.clone, body=%wide.region_4.5_spmd.clone.sunk | while | flops 1576967 | bytes 614565 | solution.py:146
  274.5 4.9 %convolution_bitcast_fusion.12 = f32[5,5,4,128]{1,0,3,2:T(8,128)} fusion(f32[5,5,4,128]{1,0,3,2:T(8,128)S(1)} %copy.604, f32[5,5,4,128]{1,0,3,2:T(8,128)S(1)} %copy.649), kind=kOutput, calls=%fused_computation.24.clone.1 | convolution fusion | flops 768000 | bytes 153600 | tf_op jit(solution)/shard_map/while/body/eval_jaxpr/ijap,jkap->ikap/dot_general | solution.py:143
  282.0 4.9 %convolution_bitcast_fusion.12 = f32[5,5,4,128]{1,0,3,2:T(8,128)} fusion(f32[5,5,4,128]{1,0,3,2:T(8,128)S(1)} %copy.604, f32[5,5,4,128]{1,0,3,2:T(8,128)S(1)} %copy.649), kind=kOutput, calls=%fused_computation.24.clone.1 | convolution fusion | flops 768000 | bytes 153600 | tf_op jit(solution)/shard_map/while/body/eval_jaxpr/ijap,jkap->ikap/dot_general | solution.py:143
  297.0 4.9 %convolution_bitcast_fusion.12 = f32[5,5,4,128]{1,0,3,2:T(8,128)} fusion(f32[5,5,4,128]{1,0,3,2:T(8,128)S(1)} %copy.604, f32[5,5,4,128]{1,0,3,2:T(8,128)S(1)} %copy.649), kind=kOutput, calls=%fused_computation.24.clone.1 | convolution fusion | flops 768000 | bytes 153600 | tf_op jit(solution)/shard_map/while/body/eval_jaxpr/ijap,jkap->ikap/dot_general | solution.py:143
  312.0 4.9 %convolution_bitcast_fusion.12 = f32[5,5,4,128]{1,0,3,2:T(8,128)} fusion(f32[5,5,4,128]{1,0,3,2:T(8,128)S(1)} %copy.604, f32[5,5,4,128]{1,0,3,2:T(8,128)S(1)} %copy.649), kind=kOutput, calls=%fused_computation.24.clone.1 | convolution fusion | flops 768000 | bytes 153600 | tf_op jit(solution)/shard_map/while/body/eval_jaxpr/ijap,jkap->ikap/dot_general | solution.py:143
  327.0 4.9 %convolution_bitcast_fusion.12 = f32[5,5,4,128]{1,0,3,2:T(8,128)} fusion(f32[5,5,4,128]{1,0,3,2:T(8,128)S(1)} %copy.604, f32[5,5,4,128]{1,0,3,2:T(8,128)S(1)} %copy.649), kind=kOutput, calls=%fused_computation.24.clone.1 | convolution fusion | flops 768000 | bytes 153600 | tf_op jit(solution)/shard_map/while/body/eval_jaxpr/ijap,jkap->ikap/dot_general | solution.py:143
  334.0 12.6 %all-gather.2 = f32[480,128]{1,0:T(8,128)S(1)} all-gather(f32[120,128]{1,0:T(8,128)S(1)} %pad_maximum_fusion.7), channel_id=4, replica_groups=mesh['pitch'=8,'span_0'=8,'span_1'=4] {'span_1'}, dimensions={0}, use_global_device_ids=true | all-gather | bytes 307200 | tf_op jit(solution)/shard_map/all_gather | solution.py:42
  354.8 5.1 %fusion.77 = f32[4,128,5,5]{3,2,1,0:T(8,128)S(1)} fusion(f32[5,5,4,128]{1,0,3,2:T(8,128)} %copy.222, f32[5,5]{0,1:T(8,128)S(1)} %fusion.105), kind=kOutput, calls=%fused_computation.94 | convolution fusion | flops 768000 | bytes 102500 | tf_op jit(solution)/shard_map/ijap,jkap->ikap/dot_general | solution.py:121
  369.0 4.9 %fusion.49 = f32[5,5,4,128]{0,1,3,2:T(8,128)} fusion(f32[5,5,4,128]{1,0,3,2:T(8,128)S(1)} %copy-done.10, f32[4,128,5,5]{3,2,1,0:T(8,128)S(1)} %fusion.26), kind=kOutput, calls=%fused_computation.77 | convolution fusion | flops 768000 | bytes 153600 | tf_op jit(solution)/shard_map/ijap,jkap->ikap/dot_general | solution.py:121
  375.9 25.4 %all-gather.3 = f32[960,128]{1,0:T(8,128)S(1)} all-gather(f32[120,128]{1,0:T(8,128)S(1)} %pad_maximum_fusion.8), channel_id=5, replica_groups=mesh['pitch'=8,'span_0'=8,'span_1'=4] {'span_0'}, dimensions={0}, use_global_device_ids=true | all-gather | bytes 552960 | tf_op jit(solution)/shard_map/all_gather | solution.py:42
  402.1 6.2 %multiply_reduce_fusion.2 = f32[4,128,5]{2,1,0:T(8,128)S(1)} fusion(f32[5,5,4,128]{0,1,3,2:T(8,128)} %fusion.49, f32[4,128,5,5]{3,2,1,0:T(8,128)} %copy-done.4, f32[4,128,5,5]{3,2,1,0:T(8,128)} %copy-done.2, f32[4,128,5,5]{3,2,1,0:T(8,128)S(1)} %fusion.77, f32[4,128,5]{2,1,0:T(8,128)S(1)} %copy.544, f32[5,5]{0,1:T(8,128)S(1)} %fusion.105, pred[]{:T(512)S(6)} %lt.146, ...), kind=kOutput, calls=%fused_computation.71 | convolution fusion | flops 842240 | bytes 225384 | tf_op jit(solution)/shard_map/ijap,jkap->ikap/dot_general | solution.py:121
  409.5 10.8 %while.69 = (s32[]{:T(128)}, f32[5,4,128]{2,1,0:T(4,128)S(1)}, f32[5,4,8,128]{3,2,1,0:T(8,128)S(1)}, f32[5,4,8,128]{3,2,1,0:T(8,128)S(1)}, f32[5,5]{1,0:T(8,128)...) while((s32[]{:T(128)}, f32[5,4,128]{2,1,0:T(4,128)S(1)}, ...), condition=%wide.region_7.8_spmd, body=%wide.region_6.7_spmd.sunk | while | flops 179206 | bytes 286979 | solution.py:164
  (474 shorter events, 186.8 us)
Async XLA Ops:
  0.0 11.8 %copy-start.16 = (s32[2]{0:T(128)S(1)}, s32[2]{0:T(128)}, u32[]{:S(2)}) copy-start(s32[2]{0:T(128)} %param.23) | copy-start | bytes 28
  0.0 12.2 %copy-start.11 = (f32[5,5,4,8,128]{4,3,2,1,0:T(8,128)S(1)}, f32[5,5,4,8,128]{4,3,2,1,0:T(8,128)}, u32[]{:S(2)}) copy-start(f32[5,5,4,8,128]{4,3,2,1,0:T(8,128)} %param.19) | copy-start | bytes 1228804
  1.7 10.8 %all-to-all-start = ((f32[2,5,8,128]{3,0,1,2:T(2,128)}), f32[2,5,8,128]{3,0,1,2:T(2,128)S(1)}, u32[]{:S(2)}, u32[]{:S(2)}) async-start(f32[2,5,8,128]{3,0,1,2:T(2,128)} %copy.183), calls=%async_computation | async-start | bytes 81920 | tf_op jit(solution)/shard_map/all_to_all | solution.py:171
  8.9 62.3 %collective-permute-start.1 = (f32[5,4,8,1]{3,0,2,1:T(8,128)S(1)}, f32[5,4,8,1]{3,0,2,1:T(8,128)S(1)}, u32[]{:S(2)}, u32[]{:S(2)}) collective-permute-start(f32[5,4,8,1]{3,0,2,1:T(8,128)S(1)} %get-tuple-element.817), channel_id=1, source_target_pairs={{32,0},{64,32},{96,64},{128,96},{160,128},{192,160},{224,192},{0,2... | collective-permute-start | bytes 1928 | tf_op jit(solution)/shard_map/ppermute | solution.py:23
  9.0 70.2 %collective-permute-start = (f32[5,4,8,1]{3,0,2,1:T(8,128)}, f32[5,4,8,1]{3,0,2,1:T(8,128)}, u32[]{:S(2)}, u32[]{:S(2)}) collective-permute-start(f32[5,4,8,1]{3,0,2,1:T(8,128)} %get-tuple-element.816), channel_id=1, source_target_pairs={{0,32},{32,64},{64,96},{96,128},{128,160},{160,192},{192,224},{224... | collective-permute-start | bytes 1928 | tf_op jit(solution)/shard_map/ppermute | solution.py:22
  12.2 69.1 %copy-start.14 = (f32[5,5]{1,0:T(8,128)}, f32[5,5]{1,0:T(8,128)S(1)}, u32[]{:S(2)}) copy-start(f32[5,5]{1,0:T(8,128)S(1)} %copy.519) | copy-start | bytes 304
  64.4 10.7 %all-to-all-start.1 = ((f32[8,1,1280]{2,1,0:T(1,128)}), f32[8,1,1280]{2,1,0:T(1,128)S(1)}, u32[]{:S(2)}, u32[]{:S(2)}) async-start(f32[8,1,1280]{2,1,0:T(1,128)} %reshape.404), calls=%async_computation.1 | async-start | bytes 81920 | tf_op jit(solution)/shard_map/all_to_all | solution.py:178
  84.9 3.6 copy-start
  95.6 3.6 copy-start
  106.4 3.6 copy-start
  117.1 3.6 copy-start
  127.8 3.6 copy-start
  138.6 3.6 copy-start
  149.3 3.6 copy-start
  160.0 3.6 copy-start
  192.3 5.1 %copy-start.5 = (f32[5,5,4,128]{1,0,3,2:T(8,128)S(1)}, f32[5,5,4,128]{1,0,3,2:T(8,128)}, u32[]{:S(2)}) copy-start(f32[5,5,4,128]{1,0,3,2:T(8,128)} %copy.212) | copy-start | bytes 153604
  197.5 3.7 copy-start.7
  201.2 3.9 copy-start.1
  201.2 5.3 %copy-start.9 = (f32[5,5,4,128]{1,0,3,2:T(8,128)S(1)}, f32[5,5,4,128]{1,0,3,2:T(8,128)}, u32[]{:S(2)}) copy-start(f32[5,5,4,128]{1,0,3,2:T(8,128)} %copy.214) | copy-start | bytes 153604
  205.2 1.4 copy-start.3
  252.6 6.3 %copy-start.13 = (f32[4,128,5]{1,0,2:T(4,128)S(1)}, f32[4,128,5]{1,0,2:T(4,128)}, u32[]{:S(2)}) copy-start(f32[4,128,5]{1,0,2:T(4,128)} %get-tuple-element.760) | copy-start | bytes 30724
  258.8 11.7 %copy-start.15 = (f32[5,5]{1,0:T(8,128)S(1)}, f32[5,5]{1,0:T(8,128)}, u32[]{:S(2)}) copy-start(f32[5,5]{1,0:T(8,128)} %copy-done.14) | copy-start | bytes 304
  354.8 5.2 %copy-start.6 = (f32[5,5,4,128]{1,0,3,2:T(8,128)S(1)}, f32[5,5,4,128]{1,0,3,2:T(8,128)}, u32[]{:S(2)}) copy-start(f32[5,5,4,128]{1,0,3,2:T(8,128)} %copy.223) | copy-start | bytes 153604
  360.0 3.7 copy-start.8
  363.7 3.9 copy-start.2
  363.7 5.2 %copy-start.10 = (f32[5,5,4,128]{1,0,3,2:T(8,128)S(1)}, f32[5,5,4,128]{1,0,3,2:T(8,128)}, u32[]{:S(2)}) copy-start(f32[5,5,4,128]{1,0,3,2:T(8,128)} %copy.225) | copy-start | bytes 153604
  367.7 1.3 copy-start.4
  420.3 0.6 copy-start.12
where the time goes:
time: 427 us; the launch traced here: 421 us
  matrix products  212 us (50%)
  local copies, waits for them, and re-layouts  106 us (25%)
  blocking collectives  79.3 us (19%)
  starting transfers between devices  12.7 us (3%)
  other arithmetic  5.2 us (1%)
    all_gather x4, blocking collectives, collected_together(): both, at, found = (lax.all_gather(jnp.concatenate(lines), axis), 0, {})  79.3 us
    dot_general x16, matrix products, compose(): maps = jnp.einsum('ijap,jkap->ikap', factor, maps, precision=highest)  78.4 us
    dot_general x10, matrix products, chain_maps(): jnp.einsum('ijap,jkap->ikap', trailing_maps, early_maps, precision=highest)  47.7 us
    dot_general x8, matrix products, apply_block(): return jnp.einsum('ijap,jap->iap', block, vector, precision=highest)  28.6 us
    squeeze x56, local copies, waits for them, and re-layouts, entering(): total = combine(total, jax.tree.map(lambda part: part[k], pieces))  24.8 us
    dot_general x1, matrix products, inverse_dft(): jnp.dot(flat_imag, sine.T, precision=highest)  20.6 us
    dynamic_slice x16, local copies, waits for them, and re-layouts, advance(): lax.dynamic_index_in_dim(inverse_diagonal, row_index, 3, keepdims=False)  16.8 us
    while x64, local copies, waits for them, and re-layouts  14.1 us
  transfers between devices with their start and end apart: 4, of which 1 were waited for; matrix products, arithmetic and copies ran while one was open for 14% of the time, Pallas kernels for 0%

commit v1 on v0

v1 whole, which is shorter than its diff:
```python
import jax
import jax.numpy as jnp
import numpy as np
from jax import lax
from jax.experimental import pallas as pl
from jax.experimental.pallas import tpu as pltpu
from jax.sharding import PartitionSpec as P

NP = 1024
PITCH = 8
GROUP = 4
LAYERS = 8
V = 5
LINE = 16
MAPS = 80
VECS = 16
LANES = 128
HIGHEST = lax.Precision.HIGHEST

SPREAD, TWIDDLE, FORWARD, BACK_RE, BACK_IM, GATHER_RE, GATHER_IM = np.cumsum([0, 160, 16, 256, 128, 128, 128]).tolist()


def table():
    two_pi = 2.0 * np.pi
    a = np.arange(8)
    b = np.arange(128)
    k2 = np.arange(64)
    eight = two_pi * (np.outer(a, a) % 8) / 8
    spread = np.zeros((2, 10, 8, 8, LINE))
    for line in range(10):
        spread[0, line, :, :, line] = np.cos(eight)
        spread[1, line, :, :, line] = -np.sin(eight)
    twiddle = two_pi * np.outer(a, b) / NP
    lanes = two_pi * (np.outer(b, k2) % 128) / 128
    cos, sin = np.cos(lanes), np.sin(lanes)
    forward = np.block([[cos, -sin], [sin, cos]])
    back_re = np.concatenate([cos.T, -sin.T], 0)
    back_im = np.concatenate([sin.T, cos.T], 0)
    gather_re = np.zeros((8, LINE, 16, 8))
    gather_im = np.zeros((8, LINE, 16, 8))
    for line in range(10):
        gather_re[:, line, line, :] = np.cos(eight)
        gather_im[:, line, line, :] = -np.sin(eight)
    parts = [
        spread.reshape(160, 128),
        np.cos(twiddle),
        np.sin(twiddle),
        forward,
        back_re,
        back_im,
        gather_re.reshape(128, 128),
        gather_im.reshape(128, 128),
    ]
    return np.concatenate(parts, 0).astype(np.float32)


def every(start, stride):
    return pl.ds(start, 8, stride=stride)


def rows(start, size):
    return pl.ds(pl.multiple_of(start, 8), size)


def product(later, earlier):
    total = later[0][None] * earlier[:, 0][:, None]
    for j in range(1, V):
        total = total + later[j][None] * earlier[:, j][:, None]
    return total


def apply(matrix, vector):
    total = matrix[0] * vector[0][None]
    for j in range(1, V):
        total = total + matrix[j] * vector[j][None]
    return total


def scaled(block, coupling, which):
    columns = []
    for k in range(V):
        total = block[:, 0] * (-coupling[which, k])
        for j in range(1, V):
            total = total + block[:, j] * (-coupling[which, j * V + k])
        columns.append(total)
    return jnp.stack(columns)


def kernel(
    residual, inverse, prior, coupling, characteristic, cutoffs, const, out,
    lower, upper, planes_out, planes_in, corr_out, corr_in,
    maps_out, maps_in, layer_maps, vecs_out, vecs_in, layer_vecs, entry_out, entry_in,
    down, up, first, second, third, source, base, flat, spectra,
    pitch_s, pitch_r, back_s, back_r, side_s, side_r,
    gm_s, gm_r, zm_s, zm_r, gv_s, gv_r, zv_s, zv_r, ge_s, ge_r,
):
    pitch = lax.axis_index("pitch")
    span = lax.axis_index("span")
    layer = span // GROUP
    member = span % GROUP

    def at_pitch(d):
        return {"pitch": lax.rem(pitch + d, PITCH), "span": span}

    def at_member(d):
        return {"pitch": pitch, "span": layer * GROUP + lax.rem(member + d, GROUP)}

    def at_layer(d):
        return {"pitch": pitch, "span": lax.rem(layer + d, LAYERS) * GROUP + member}

    peers = [at_pitch(d) for d in range(1, PITCH)]
    peers += [at_member(d) for d in range(1, GROUP)]
    peers += [at_layer(d) for d in range(1, LAYERS)]
    barrier = pltpu.get_barrier_semaphore()
    for peer in peers:
        pl.semaphore_signal(barrier, inc=1, device_id=peer, device_id_type=pl.DeviceIdType.MESH)

    def send(src, dst, send_sem, recv_sem, peer):
        copy = pltpu.make_async_remote_copy(
            src_ref=src, dst_ref=dst, send_sem=send_sem, recv_sem=recv_sem,
            device_id=peer, device_id_type=pl.DeviceIdType.MESH,
        )
        copy.start()
        return copy

    planes_out[...] = jnp.zeros_like(planes_out)
    for q, axial in enumerate((0, GROUP - 1)):
        for j in range(V):
            planes_out[every(q * V + j, LINE), :] = residual[j, axial * 8 : axial * 8 + 8, :]

    maps_out[...] = jnp.zeros_like(maps_out)
    vecs_out[...] = jnp.zeros_like(vecs_out)
    reach = None
    for s in range(4):
        block = inverse[:, :, every(s, 4), :]
        down[s] = scaled(block, coupling, 0)
        up[s] = scaled(block, coupling, 1)
        reach = down[s] if s == 0 else product(down[s], reach)
        first[s] = reach
    for k in range(V):
        for i in range(V):
            maps_out[every(8 * k + i, MAPS), :] = reach[k, i]
    both = reach
    trail = up[3]
    second[3] = both
    third[3] = trail
    for s in (2, 1, 0):
        both = first[s] + product(up[s], both)
        trail = product(up[s], trail)
        second[s] = both
        third[s] = trail
    for k in range(V):
        for i in range(V):
            maps_out[every(40 + 8 * k + i, MAPS), :] = trail[k, i]
            maps_out[every(8 * k + 5 + i if i < 3 else 40 + 8 * k + 2 + i, MAPS), :] = both[k, i]

    pl.semaphore_wait(barrier, len(peers))

    pitch_copies = []
    for d in range(1, PITCH):
        to = lax.rem(pitch + d, PITCH)
        pitch_copies.append(send(
            planes_out.at[rows(to * LINE, LINE)], planes_in.at[rows(pitch * LINE, LINE)],
            pitch_s.at[d], pitch_r.at[d], at_pitch(d),
        ))
    side_copies = [
        send(prior, lower, side_s.at[0], side_r.at[0], at_pitch(1)),
        send(prior, upper, side_s.at[1], side_r.at[1], at_pitch(PITCH - 1)),
    ]
    map_copies = []
    for d in range(1, GROUP):
        to = lax.rem(member + d, GROUP)
        map_copies.append(send(
            maps_out.at[rows(to * 2 * MAPS, 2 * MAPS)], maps_in.at[rows(member * 2 * MAPS, 2 * MAPS)],
            gm_s.at[d], gm_r.at[d], at_member(d),
        ))
    planes_in[rows(pitch * LINE, LINE), :] = planes_out[rows(pitch * LINE, LINE), :]
    maps_in[rows(member * 2 * MAPS, 2 * MAPS), :] = maps_out[rows(member * 2 * MAPS, 2 * MAPS), :]

    flat[100:104, :] = jnp.zeros((4, 512), jnp.float32)
    for n in range(50):
        flat[2 * n : 2 * n + 2, :] = characteristic[n]
    whole = flat[...]
    high = whole.astype(jnp.bfloat16)
    rest = whole - high.astype(jnp.float32)
    middle = rest.astype(jnp.bfloat16)
    low = (rest - middle.astype(jnp.float32)).astype(jnp.bfloat16)
    harmonic = lax.broadcasted_iota(jnp.int32, (512, LANES), 0)
    lane = lax.broadcasted_iota(jnp.int32, (512, LANES), 1)
    apart = harmonic - 8 * (lane % 64)
    for k1 in range(8):
        pick = jnp.where(apart == k1, 1.0, 0.0).astype(jnp.bfloat16)
        part = jnp.dot(high, pick, preferred_element_type=jnp.float32)
        part = part + jnp.dot(middle, pick, preferred_element_type=jnp.float32)
        part = part + jnp.dot(low, pick, preferred_element_type=jnp.float32)
        spectra[pl.ds(k1, 104, stride=8), :] = part

    for copy in side_copies:
        copy.wait_recv()
    column = lax.broadcasted_iota(jnp.int32, (V, 32, LANES), 2)
    own = prior[...]
    below = pltpu.roll(jnp.where(column == LANES - 1, lower[...], own), 1, 2)
    above = pltpu.roll(jnp.where(column == 0, upper[...], own), LANES - 1, 2)
    zero_row = jnp.zeros((8, LANES), jnp.float32)
    for i in range(V):
        total = residual[i]
        before = after = None
        for j in range(V):
            total = total - coupling[2, i * V + j] * below[j] - coupling[3, i * V + j] * above[j]
            low_term = coupling[4, i * V + j] * own[j]
            high_term = coupling[5, i * V + j] * own[j]
            before = low_term if before is None else before + low_term
            after = high_term if after is None else after + high_term
        total = total - jnp.concatenate([zero_row, before[:24]], 0) - jnp.concatenate([after[8:], zero_row], 0)
        source[i] = total

    for copy in pitch_copies:
        copy.wait_recv()
    spread = jnp.dot(
        const[SPREAD : SPREAD + 160, :], planes_in[...], precision=HIGHEST, preferred_element_type=jnp.float32
    ).reshape(2, 10, 8, LANES)
    turn_re = const[TWIDDLE : TWIDDLE + 8, :][None]
    turn_im = const[TWIDDLE + 8 : TWIDDLE + 16, :][None]
    turned_re = (spread[0] * turn_re + spread[1] * turn_im).reshape(80, LANES)
    turned_im = (spread[1] * turn_re - spread[0] * turn_im).reshape(80, LANES)
    spectrum = jnp.dot(
        jnp.concatenate([turned_re, turned_im], 1), const[FORWARD : FORWARD + 256, :],
        precision=HIGHEST, preferred_element_type=jnp.float32,
    )
    number = lax.broadcasted_iota(jnp.int32, (8, LANES), 0) + 8 * (lax.broadcasted_iota(jnp.int32, (8, LANES), 1) % 64)
    weight = jnp.where(number == 0, 1.0, 2.0) / NP
    sign = jnp.where(lax.broadcasted_iota(jnp.int32, (80, LANES), 1) < 64, -1.0, 1.0)
    crossed = (pltpu.roll(spectrum, 64, 1) * sign).reshape(2, V, 8, LANES)
    spectrum = spectrum.reshape(2, V, 8, LANES)
    corrected = []
    for q in range(2):
        factor = jnp.where(number < cutoffs[q], weight, 0.0)
        for i in range(V):
            total = None
            for j in range(V):
                row = (q * 25 + i * V + j) * 16
                term = spectra[row : row + 8, :] * spectrum[q, j] + spectra[row + 8 : row + 16, :] * crossed[q, j]
                total = term if total is None else total + term
            corrected.append(total * factor)
    corrected = jnp.concatenate(corrected, 0)
    back_re = jnp.dot(
        corrected, const[BACK_RE : BACK_RE + 128, :], precision=HIGHEST, preferred_element_type=jnp.float32
    ).reshape(10, 8, LANES)
    back_im = jnp.dot(
        corrected, const[BACK_IM : BACK_IM + 128, :], precision=HIGHEST, preferred_element_type=jnp.float32
    ).reshape(10, 8, LANES)
    filler = jnp.zeros((48, LANES), jnp.float32)
    lines_re = jnp.concatenate([(back_re * turn_re - back_im * turn_im).reshape(80, LANES), filler], 0)
    lines_im = jnp.concatenate([(back_im * turn_re + back_re * turn_im).reshape(80, LANES), filler], 0)
    corr_out[...] = jnp.dot(
        const[GATHER_RE : GATHER_RE + 128, :], lines_re, precision=HIGHEST, preferred_element_type=jnp.float32
    ) + jnp.dot(
        const[GATHER_IM : GATHER_IM + 128, :], lines_im, precision=HIGHEST, preferred_element_type=jnp.float32
    )
    back_copies = []
    for d in range(1, PITCH):
        to = lax.rem(pitch + d, PITCH)
        back_copies.append(send(
            corr_out.at[rows(to * LINE, LINE)], corr_in.at[rows(pitch * LINE, LINE)],
            back_s.at[d], back_r.at[d], at_pitch(d),
        ))
    corr_in[rows(pitch * LINE, LINE), :] = corr_out[rows(pitch * LINE, LINE), :]

    place = lax.broadcasted_iota(jnp.int32, (8, LANES), 0)

    def tiles(ref, n, second_half):
        start = n * MAPS + (40 if second_half else 0)
        return [ref[start + 8 * j : start + 8 * j + 8, :] for j in range(V)]

    def spread_rows(vector):
        return [jnp.broadcast_to(vector[..., j : j + 1, :], vector.shape) for j in range(V)]

    def mix(matrix, parts):
        total = matrix[0] * parts[0]
        for j in range(1, V):
            total = total + matrix[j] * parts[j]
        return total

    def moved(top, bottom):
        axis = top.ndim - 2
        return jnp.where(place < 3, pltpu.roll(top, 3, axis), pltpu.roll(bottom, 6, axis))

    for copy in map_copies:
        copy.wait_recv()
    top = maps_in[0:40, :].reshape(V, 8, LANES)
    bottom = maps_in[40:80, :].reshape(V, 8, LANES)
    across = [moved(top, bottom)]
    forward = top
    for n in range(1, 8):
        parts = spread_rows(forward)
        forward = mix(tiles(maps_in, n, False), parts)
        across.append(moved(forward, mix(tiles(maps_in, n, True), parts)))
    backward = jnp.concatenate([maps_in[7 * MAPS + 40 : 8 * MAPS, :].reshape(V, 8, LANES), across[7]], 0)
    for n in range(6, -1, -1):
        backward = mix(tiles(maps_in, n, True), spread_rows(backward))
        backward = jnp.concatenate([backward[:V], backward[V:] + across[n]], 0)
    mine = pl.multiple_of(layer * MAPS, 8)
    whole_top = jnp.where(place < V, forward, pltpu.roll(backward[V:], 5, 1))
    whole_bottom = jnp.where(place < V, backward[:V], pltpu.roll(backward[V:], 2, 1))
    layer_maps[pl.ds(mine, 40), :] = whole_top.reshape(40, LANES)
    layer_maps[pl.ds(pl.multiple_of(layer * MAPS + 40, 8), 40), :] = whole_bottom.reshape(40, LANES)
    layer_copies = []
    for d in range(1, LAYERS):
        layer_copies.append(send(
            layer_maps.at[rows(layer * MAPS, MAPS)], layer_maps.at[rows(layer * MAPS, MAPS)],
            zm_s.at[d], zm_r.at[d], at_layer(d),
        ))

    for copy in back_copies:
        copy.wait_recv()
    for j in range(V):
        source[j, 0:8, :] = source[j, 0:8, :] + corr_in[every(j, LINE), :]
        source[j, 24:32, :] = source[j, 24:32, :] + corr_in[every(V + j, LINE), :]
    star = None
    for s in range(4):
        block = inverse[:, :, every(s, 4), :]
        rhs = source[:, every(s, 4), :]
        value = block[:, 0] * rhs[0][None]
        for j in range(1, V):
            value = value + block[:, j] * rhs[j][None]
        star = value if s == 0 else value + apply(down[s], star)
        base[s] = star
    for i in range(V):
        vecs_out[every(i, VECS), :] = star[i]
    update = star
    for s in (2, 1, 0):
        update = base[s] + apply(up[s], update)
        base[s] = update
    for i in range(V):
        vecs_out[every(8 + i, VECS), :] = update[i]
    vec_copies = []
    for d in range(1, GROUP):
        to = lax.rem(member + d, GROUP)
        vec_copies.append(send(
            vecs_out.at[rows(to * 2 * VECS, 2 * VECS)], vecs_in.at[rows(member * 2 * VECS, 2 * VECS)],
            gv_s.at[d], gv_r.at[d], at_member(d),
        ))
    vecs_in[rows(member * 2 * VECS, 2 * VECS), :] = vecs_out[rows(member * 2 * VECS, 2 * VECS), :]

    def chain(maps_ref, vecs_ref, x, y):
        entering_x, entering_y, crossing = [], [None] * 8, []
        for n in range(8):
            entering_x.append(x)
            offset = vecs_ref[n * VECS : n * VECS + 8, :]
            if x is None:
                crossing.append(vecs_ref[n * VECS + 8 : n * VECS + 16, :])
                x = offset
            else:
                parts = spread_rows(x)
                ahead = mix(tiles(maps_ref, n, False), parts)
                aside = mix(tiles(maps_ref, n, True), parts)
                crossing.append(moved(ahead, aside) + vecs_ref[n * VECS + 8 : n * VECS + 16, :])
                x = ahead + offset
        for n in range(7, -1, -1):
            entering_y[n] = y
            y = crossing[n] if y is None else mix(tiles(maps_ref, n, True), spread_rows(y)) + crossing[n]
        return entering_x, entering_y, x, y

    for copy in vec_copies:
        copy.wait_recv()
    _, _, x, y = chain(maps_in, vecs_in, None, None)
    layer_vecs[pl.ds(pl.multiple_of(layer * VECS, 8), 8), :] = x
    layer_vecs[pl.ds(pl.multiple_of(layer * VECS + 8, 8), 8), :] = y
    vec_layer_copies = []
    for d in range(1, LAYERS):
        vec_layer_copies.append(send(
            layer_vecs.at[rows(layer * VECS, VECS)], layer_vecs.at[rows(layer * VECS, VECS)],
            zv_s.at[d], zv_r.at[d], at_layer(d),
        ))
    for copy in layer_copies:
        copy.wait_recv()
    for copy in vec_layer_copies:
        copy.wait_recv()
    entering_x, entering_y, _, _ = chain(layer_maps, layer_vecs, None, None)
    x = jnp.zeros((8, LANES), jnp.float32)
    y = jnp.zeros((8, LANES), jnp.float32)
    for n in range(8):
        if entering_x[n] is not None:
            x = jnp.where(layer == n, entering_x[n], x)
        if entering_y[n] is not None:
            y = jnp.where(layer == n, entering_y[n], y)
    entering_x, entering_y, _, _ = chain(maps_in, vecs_in, x, y)
    for n in range(8):
        entry_out[n * VECS : n * VECS + 8, :] = entering_x[n]
        entry_out[n * VECS + 8 : n * VECS + 16, :] = entering_y[n]
    entry_copies = []
    for d in range(1, GROUP):
        to = lax.rem(member + d, GROUP)
        entry_copies.append(send(
            entry_out.at[rows(to * 2 * VECS, 2 * VECS)], entry_in.at[rows(member * 2 * VECS, 2 * VECS)],
            ge_s.at[d], ge_r.at[d], at_member(d),
        ))
    entry_in[rows(member * 2 * VECS, 2 * VECS), :] = entry_out[rows(member * 2 * VECS, 2 * VECS), :]
    for copy in entry_copies:
        copy.wait_recv()
    x = [entry_in[every(i, VECS), :] for i in range(V)]
    y = [entry_in[every(8 + i, VECS), :] for i in range(V)]
    for s in range(4):
        value = base[s]
        for j in range(V):
            value = value + second[s, j] * x[j][None] + third[s, j] * y[j][None]
        for i in range(V):
            out[i, every(s, 4), :] = value[i]

    for copy in pitch_copies + side_copies + map_copies + back_copies + layer_copies:
        copy.wait_send()
    for copy in vec_copies + vec_layer_copies + entry_copies:
        copy.wait_send()


def body(residual, inverse_diagonal, prior_increment, coupling, characteristic, cutoffs):
    f32 = jnp.float32
    fields = (V, 32, LANES)
    matrices = pltpu.VMEM((4, V, V, 8, LANES), f32)

    def vmem(count):
        return pltpu.VMEM((count, LANES), f32)

    def sems(count):
        return [pltpu.SemaphoreType.DMA((count,))] * 2

    scratch = [
        pltpu.VMEM(fields, f32), pltpu.VMEM(fields, f32),
        vmem(128), vmem(128), vmem(128), vmem(128),
        vmem(8 * MAPS), vmem(8 * MAPS), vmem(8 * MAPS),
        vmem(8 * VECS), vmem(8 * VECS), vmem(8 * VECS), vmem(8 * VECS), vmem(8 * VECS),
        matrices, matrices, matrices, matrices, matrices,
        pltpu.VMEM(fields, f32), pltpu.VMEM((4, V, 8, LANES), f32),
        pltpu.VMEM((104, 512), f32), vmem(104 * 8),
        *sems(PITCH), *sems(PITCH), *sems(2),
        *sems(GROUP), *sems(LAYERS), *sems(GROUP), *sems(LAYERS), *sems(GROUP),
    ]
    inside = pl.BlockSpec(memory_space=pltpu.VMEM)
    scalars = pl.BlockSpec(memory_space=pltpu.SMEM)
    result = pl.pallas_call(
        kernel,
        out_shape=jax.ShapeDtypeStruct(fields, f32),
        in_specs=[inside, inside, inside, scalars, inside, scalars, inside],
        out_specs=inside,
        scratch_shapes=scratch,
        compiler_params=pltpu.CompilerParams(collective_id=0, has_side_effects=True),
    )(
        residual.reshape(fields),
        inverse_diagonal.reshape(V, V, 32, LANES),
        prior_increment.reshape(fields),
        coupling.reshape(6, V * V),
        characteristic.transpose(0, 3, 4, 1, 2).reshape(50, 2, 512),
        cutoffs,
        jnp.asarray(table()),
    )
    return result.reshape(V, GROUP, 8, LANES)


def solution(mesh):
    field = P(None, None, "span", "pitch")
    return jax.shard_map(
        body, mesh=mesh,
        in_specs=(field, P(None, None, None, "span", "pitch"), field, P(), P(), P()),
        out_specs=field, check_vma=False,
    )
```

time: 427 us -> 35.8 us (0.08); the launches traced: 421 us -> 35.6 us
  matrix products: 212 us -> 0 us
  local copies, waits for them, and re-layouts: 106 us -> 2.93 us
  blocking collectives: 79.3 us -> 0 us
  Pallas kernels: 0 us -> 32.7 us
  starting transfers between devices: 12.7 us -> 0 us
  other arithmetic: 5.2 us -> 0 us
    dot_general x74 -> x0, matrix products: 212 us -> none  [the longest x16 78.4 us: compose(): maps = jnp.einsum('ijap,jkap->ikap', factor, maps, precision=highest)]
    all_gather x4 -> x0, blocking collectives: 79.3 us -> none  [collected_together(): both, at, found = (lax.all_gather(jnp.concatenate(lines), axis), 0, {})]
    pallas_call x0 -> x1, Pallas kernels: none -> 32.7 us  [body(): pl.pallas_call(kernel, out_shape=jax.ShapeDtypeStruct(fields, f32), in_sp...]
    squeeze x58 -> x0, local copies, waits for them, and re-layouts: 25 us -> none  [the longest x56 24.8 us: entering(): total = combine(total, jax.tree.map(lambda part: part[k], pieces))]
    dynamic_slice x40 -> x0, local copies, waits for them, and re-layouts: 24.2 us -> none  [the longest x16 16.8 us: advance(): lax.dynamic_index_in_dim(inverse_diagonal, row_index, 3, keepdims=False)]
    while x68 -> x0, local copies, waits for them, and re-layouts: 18.8 us -> none
    all_to_all x2 -> x0, starting transfers between devices: 12.2 us -> none  [the longest x1 6.71 us: body(): lax.all_to_all(line_correction, 'pitch', split_axis=3, concat_axis=2, til...]
    neg x16 -> x0, local copies, waits for them, and re-layouts: 11.3 us -> none  [compose(): factor = -jnp.einsum('ijap,jk->ikap', block, matrix, precision=highest)]
  transfers between devices with their start and end apart: 4 -> 0, of which waited for: 1 -> 0; matrix products, arithmetic and copies ran while one was open for 14% -> 0% of each run, Pallas kernels for 0% -> 0%
where the time goes in v1:
time: 35.8 us; the launch traced here: 35.6 us
  Pallas kernels  32.7 us (91%)
  local copies, waits for them, and re-layouts  2.93 us (8%)
    pallas_call x1, Pallas kernels, body(): pl.pallas_call(kernel, out_shape=jax.ShapeDtypeStruct(fields, f32), in_sp...  32.7 us
    unnamed x2, local copies, waits for them, and re-layouts  2.26 us

profile of v1, /device:TPU:2, one launch (start us, length us, event | category | flops | bytes accessed | tf_op | source)
XLA Modules:
  0.0 35.6 jit_solution(5089806912314286950)
XLA Ops:
  0.0 0.7 %copy.9 = f32[6,5,5]{2,1,0:T(8,128)S(1)} copy(f32[6,5,5]{2,0,1:T(8,128)} %param.10) | data formatting | bytes 1200 | tf_op args[3]
  0.7 0.7 %reshape.21.coupling = f32[6,25]{1,0:T(8,128)} reshape(f32[6,5,5]{2,1,0:T(8,128)S(1)} %copy.9) | data formatting | bytes 1200 | tf_op jit(solution)/shard_map/reshape | solution.py:451
  1.4 32.7 %shard_map.73 = f32[5,32,128]{2,1,0:T(8,128)} custom-call(f32[5,32,128]{2,1,0:T(8,128)} %bitcast.10, f32[5,5,32,128]{3,2,1,0:T(8,128)} %bitcast.7, f32[5,32,128]{2,1,0:T(8,128)} %bitcast.11, f32[6,25]{1,0:T(8,128)} %reshape.21.coupling, f32[50,2,512]{2,1,0:T(2,128)} %bitcast.9, s32[2]{0:T(128)} %cutoffs.1, f32[944,128]{1,0:T(8,128)} %constant.2.clone.const), custom_call_target="tpu_custom_call" | custom-call | tf_op jit(solution)/shard_map/pallas_call | solution.py:440
  34.1 1.5 %copy.11 = f32[5,4,8,128]{3,2,1,0:T(8,128)} copy(f32[5,4,8,128]{3,2,1,0:T(8,128)} %bitcast.8) | data formatting | bytes 163840

commit v2 on v1

--- a/solution.py
+++ b/solution.py
@@ -15,9 +15,8 @@
 MAPS = 80
 VECS = 16
 LANES = 128
-HIGHEST = lax.Precision.HIGHEST
-
-SPREAD, TWIDDLE, FORWARD, BACK_RE, BACK_IM, GATHER_RE, GATHER_IM = np.cumsum([0, 160, 16, 256, 128, 128, 128]).tolist()
+
+SPREAD, FORWARD, BACK_RE, BACK_IM, GATHER_RE, GATHER_IM, LOW = np.cumsum([0, 160, 256, 128, 128, 128, 128]).tolist()
 
 
 def table():
@@ -43,15 +42,17 @@
         gather_im[:, line, line, :] = -np.sin(eight)
     parts = [
         spread.reshape(160, 128),
-        np.cos(twiddle),
-        np.sin(twiddle),
         forward,
         back_re,
         back_im,
         gather_re.reshape(128, 128),
         gather_im.reshape(128, 128),
     ]
-    return np.concatenate(parts, 0).astype(np.float32)
+    whole = np.concatenate(parts, 0).astype(np.float32)
+    high = whole.astype(jnp.bfloat16)
+    low = (whole - high.astype(np.float32)).astype(jnp.bfloat16)
+    turns = np.concatenate([np.cos(twiddle), np.sin(twiddle)], 0).astype(np.float32)
+    return np.concatenate([high, low], 0), turns
 
 
 def every(start, stride):
@@ -79,16 +80,30 @@
 def scaled(block, coupling, which):
     columns = []
     for k in range(V):
-        total = block[:, 0] * (-coupling[which, k])
+        total = block[:, 0] * (-coupling[0, which, k])
         for j in range(1, V):
-            total = total + block[:, j] * (-coupling[which, j * V + k])
+            total = total + block[:, j] * (-coupling[j, which, k])
         columns.append(total)
     return jnp.stack(columns)
 
 
+def times(data, const, start, size, left=False):
+    data_high = data.astype(jnp.bfloat16)
+    data_low = (data - data_high.astype(jnp.float32)).astype(jnp.bfloat16)
+    high = const[start : start + size, :]
+    low = const[LOW + start : LOW + start + size, :]
+    pairs = ((data_high, high), (data_low, high), (data_high, low))
+    total = None
+    for x, w in pairs:
+        part = jnp.dot(w, x, preferred_element_type=jnp.float32) if left else jnp.dot(x, w, preferred_element_type=jnp.float32)
+        total = part if total is None else total + part
+    return total
+
+
 def kernel(
-    residual, inverse, prior, coupling, characteristic, cutoffs, const, out,
-    lower, upper, planes_out, planes_in, corr_out, corr_in,
+    residual_in, inverse_in, prior_in, coupling, characteristic_in, cutoffs, const_in, turns_in, out,
+    residual, inverse, prior, characteristic, const, turns, load_s,
+    lower, upper, edge_low, edge_high, planes_out, planes_in, corr_out, corr_in,
     maps_out, maps_in, layer_maps, vecs_out, vecs_in, layer_vecs, entry_out, entry_in,
     down, up, first, second, third, source, base, flat, spectra,
     pitch_s, pitch_r, back_s, back_r, side_s, side_r,
@@ -115,6 +130,14 @@
     for peer in peers:
         pl.semaphore_signal(barrier, inc=1, device_id=peer, device_id_type=pl.DeviceIdType.MESH)
 
+    loads = []
+    for n, (src, dst) in enumerate((
+        (residual_in, residual), (prior_in, prior), (inverse_in, inverse),
+        (characteristic_in, characteristic), (const_in, const), (turns_in, turns),
+    )):
+        loads.append(pltpu.make_async_copy(src, dst, load_s.at[n]))
+        loads[-1].start()
+
     def send(src, dst, send_sem, recv_sem, peer):
         copy = pltpu.make_async_remote_copy(
             src_ref=src, dst_ref=dst, send_sem=send_sem, recv_sem=recv_sem,
@@ -124,12 +147,37 @@
         return copy
 
     planes_out[...] = jnp.zeros_like(planes_out)
+    maps_out[...] = jnp.zeros_like(maps_out)
+    vecs_out[...] = jnp.zeros_like(vecs_out)
+    loads[0].wait()
     for q, axial in enumerate((0, GROUP - 1)):
         for j in range(V):
             planes_out[every(q * V + j, LINE), :] = residual[j, axial * 8 : axial * 8 + 8, :]
 
-    maps_out[...] = jnp.zeros_like(maps_out)
-    vecs_out[...] = jnp.zeros_like(vecs_out)
+    pl.semaphore_wait(barrier, len(peers))
+
+    pitch_copies = []
+    for d in range(1, PITCH):
+        to = lax.rem(pitch + d, PITCH)
+        pitch_copies.append(send(
+            planes_out.at[rows(to * LINE, LINE)], planes_in.at[rows(pitch * LINE, LINE)],
+            pitch_s.at[d], pitch_r.at[d], at_pitch(d),
+        ))
+    loads[1].wait()
+    column = lax.broadcasted_iota(jnp.int32, (8, LANES), 1)
+    last = initial = jnp.zeros((8, LANES), jnp.float32)
+    for n in range(V * GROUP):
+        tile = prior[n // GROUP, n % GROUP * 8 : n % GROUP * 8 + 8, :]
+        last = jnp.where(column == n, pltpu.roll(tile, n + 1, 1), last)
+        initial = jnp.where(column == n, pltpu.roll(tile, n, 1) if n else tile, initial)
+    edge_high[...] = last
+    edge_low[...] = initial
+    side_copies = [
+        send(edge_high, lower, side_s.at[0], side_r.at[0], at_pitch(1)),
+        send(edge_low, upper, side_s.at[1], side_r.at[1], at_pitch(PITCH - 1)),
+    ]
+
+    loads[2].wait()
     reach = None
     for s in range(4):
         block = inverse[:, :, every(s, 4), :]
@@ -154,19 +202,6 @@
             maps_out[every(40 + 8 * k + i, MAPS), :] = trail[k, i]
             maps_out[every(8 * k + 5 + i if i < 3 else 40 + 8 * k + 2 + i, MAPS), :] = both[k, i]
 
-    pl.semaphore_wait(barrier, len(peers))
-
-    pitch_copies = []
-    for d in range(1, PITCH):
-        to = lax.rem(pitch + d, PITCH)
-        pitch_copies.append(send(
-            planes_out.at[rows(to * LINE, LINE)], planes_in.at[rows(pitch * LINE, LINE)],
-            pitch_s.at[d], pitch_r.at[d], at_pitch(d),
-        ))
-    side_copies = [
-        send(prior, lower, side_s.at[0], side_r.at[0], at_pitch(1)),
-        send(prior, upper, side_s.at[1], side_r.at[1], at_pitch(PITCH - 1)),
-    ]
     map_copies = []
     for d in range(1, GROUP):
         to = lax.rem(member + d, GROUP)
@@ -177,6 +212,7 @@
     planes_in[rows(pitch * LINE, LINE), :] = planes_out[rows(pitch * LINE, LINE), :]
     maps_in[rows(member * 2 * MAPS, 2 * MAPS), :] = maps_out[rows(member * 2 * MAPS, 2 * MAPS), :]
 
+    loads[3].wait()
     flat[100:104, :] = jnp.zeros((4, 512), jnp.float32)
     for n in range(50):
         flat[2 * n : 2 * n + 2, :] = characteristic[n]
@@ -195,38 +231,16 @@
         part = part + jnp.dot(low, pick, preferred_element_type=jnp.float32)
         spectra[pl.ds(k1, 104, stride=8), :] = part
 
-    for copy in side_copies:
-        copy.wait_recv()
-    column = lax.broadcasted_iota(jnp.int32, (V, 32, LANES), 2)
-    own = prior[...]
-    below = pltpu.roll(jnp.where(column == LANES - 1, lower[...], own), 1, 2)
-    above = pltpu.roll(jnp.where(column == 0, upper[...], own), LANES - 1, 2)
-    zero_row = jnp.zeros((8, LANES), jnp.float32)
-    for i in range(V):
-        total = residual[i]
-        before = after = None
-        for j in range(V):
-            total = total - coupling[2, i * V + j] * below[j] - coupling[3, i * V + j] * above[j]
-            low_term = coupling[4, i * V + j] * own[j]
-            high_term = coupling[5, i * V + j] * own[j]
-            before = low_term if before is None else before + low_term
-            after = high_term if after is None else after + high_term
-        total = total - jnp.concatenate([zero_row, before[:24]], 0) - jnp.concatenate([after[8:], zero_row], 0)
-        source[i] = total
-
     for copy in pitch_copies:
         copy.wait_recv()
-    spread = jnp.dot(
-        const[SPREAD : SPREAD + 160, :], planes_in[...], precision=HIGHEST, preferred_element_type=jnp.float32
-    ).reshape(2, 10, 8, LANES)
-    turn_re = const[TWIDDLE : TWIDDLE + 8, :][None]
-    turn_im = const[TWIDDLE + 8 : TWIDDLE + 16, :][None]
+    loads[4].wait()
+    loads[5].wait()
+    spread = times(planes_in[...], const, SPREAD, 160, True).reshape(2, 10, 8, LANES)
+    turn_re = turns[0:8, :][None]
+    turn_im = turns[8:16, :][None]
     turned_re = (spread[0] * turn_re + spread[1] * turn_im).reshape(80, LANES)
     turned_im = (spread[1] * turn_re - spread[0] * turn_im).reshape(80, LANES)
-    spectrum = jnp.dot(
-        jnp.concatenate([turned_re, turned_im], 1), const[FORWARD : FORWARD + 256, :],
-        precision=HIGHEST, preferred_element_type=jnp.float32,
-    )
+    spectrum = times(jnp.concatenate([turned_re, turned_im], 1), const, FORWARD, 256)
     number = lax.broadcasted_iota(jnp.int32, (8, LANES), 0) + 8 * (lax.broadcasted_iota(jnp.int32, (8, LANES), 1) % 64)
     weight = jnp.where(number == 0, 1.0, 2.0) / NP
     sign = jnp.where(lax.broadcasted_iota(jnp.int32, (80, LANES), 1) < 64, -1.0, 1.0)
@@ -243,20 +257,12 @@
                 total = term if total is None else total + term
             corrected.append(total * factor)
     corrected = jnp.concatenate(corrected, 0)
-    back_re = jnp.dot(
-        corrected, const[BACK_RE : BACK_RE + 128, :], precision=HIGHEST, preferred_element_type=jnp.float32
-    ).reshape(10, 8, LANES)
-    back_im = jnp.dot(
-        corrected, const[BACK_IM : BACK_IM + 128, :], precision=HIGHEST, preferred_element_type=jnp.float32
-    ).reshape(10, 8, LANES)
+    back_re = times(corrected, const, BACK_RE, 128).reshape(10, 8, LANES)
+    back_im = times(corrected, const, BACK_IM, 128).reshape(10, 8, LANES)
     filler = jnp.zeros((48, LANES), jnp.float32)
     lines_re = jnp.concatenate([(back_re * turn_re - back_im * turn_im).reshape(80, LANES), filler], 0)
     lines_im = jnp.concatenate([(back_im * turn_re + back_re * turn_im).reshape(80, LANES), filler], 0)
-    corr_out[...] = jnp.dot(
-        const[GATHER_RE : GATHER_RE + 128, :], lines_re, precision=HIGHEST, preferred_element_type=jnp.float32
-    ) + jnp.dot(
-        const[GATHER_IM : GATHER_IM + 128, :], lines_im, precision=HIGHEST, preferred_element_type=jnp.float32
-    )
+    corr_out[...] = times(lines_re, const, GATHER_RE, 128, True) + times(lines_im, const, GATHER_IM, 128, True)
     back_copies = []
     for d in range(1, PITCH):
         to = lax.rem(pitch + d, PITCH)
@@ -310,6 +316,34 @@
             layer_maps.at[rows(layer * MAPS, MAPS)], layer_maps.at[rows(layer * MAPS, MAPS)],
             zm_s.at[d], zm_r.at[d], at_layer(d),
         ))
+
+    for copy in side_copies:
+        copy.wait_recv()
+    own = prior[...]
+    below, above = [], []
+    for i in range(V):
+        low_tiles, high_tiles = [], []
+        for a in range(GROUP):
+            n = i * GROUP + a
+            tile = prior[i, a * 8 : a * 8 + 8, :]
+            edge = pltpu.roll(lower[...], LANES - n, 1) if n else lower[...]
+            low_tiles.append(jnp.where(column == 0, edge, pltpu.roll(tile, 1, 1)))
+            edge = pltpu.roll(upper[...], LANES - 1 - n, 1)
+            high_tiles.append(jnp.where(column == LANES - 1, edge, pltpu.roll(tile, LANES - 1, 1)))
+        below.append(jnp.concatenate(low_tiles, 0))
+        above.append(jnp.concatenate(high_tiles, 0))
+    zero_row = jnp.zeros((8, LANES), jnp.float32)
+    for i in range(V):
+        total = residual[i]
+        before = after = None
+        for j in range(V):
+            total = total - coupling[i, 2, j] * below[j] - coupling[i, 3, j] * above[j]
+            low_term = coupling[i, 4, j] * own[j]
+            high_term = coupling[i, 5, j] * own[j]
+            before = low_term if before is None else before + low_term
+            after = high_term if after is None else after + high_term
+        total = total - jnp.concatenate([zero_row, before[:24]], 0) - jnp.concatenate([after[8:], zero_row], 0)
+        source[i] = total
 
     for copy in back_copies:
         copy.wait_recv()
@@ -425,7 +459,10 @@
         return [pltpu.SemaphoreType.DMA((count,))] * 2
 
     scratch = [
-        pltpu.VMEM(fields, f32), pltpu.VMEM(fields, f32),
+        pltpu.VMEM(fields, f32), pltpu.VMEM((V, V, 32, LANES), f32), pltpu.VMEM(fields, f32),
+        pltpu.VMEM((50, 2, 512), f32), pltpu.VMEM((2 * LOW, LANES), jnp.bfloat16), vmem(16),
+        pltpu.SemaphoreType.DMA((6,)),
+        vmem(8), vmem(8), vmem(8), vmem(8),
         vmem(128), vmem(128), vmem(128), vmem(128),
         vmem(8 * MAPS), vmem(8 * MAPS), vmem(8 * MAPS),
         vmem(8 * VECS), vmem(8 * VECS), vmem(8 * VECS), vmem(8 * VECS), vmem(8 * VECS),
@@ -436,11 +473,13 @@
         *sems(GROUP), *sems(LAYERS), *sems(GROUP), *sems(LAYERS), *sems(GROUP),
     ]
     inside = pl.BlockSpec(memory_space=pltpu.VMEM)
+    outside = pl.BlockSpec(memory_space=pl.ANY)
+    high_low, turns = table()
     scalars = pl.BlockSpec(memory_space=pltpu.SMEM)
     result = pl.pallas_call(
         kernel,
         out_shape=jax.ShapeDtypeStruct(fields, f32),
-        in_specs=[inside, inside, inside, scalars, inside, scalars, inside],
+        in_specs=[outside, outside, outside, scalars, outside, scalars, outside, outside],
         out_specs=inside,
         scratch_shapes=scratch,
         compiler_params=pltpu.CompilerParams(collective_id=0, has_side_effects=True),
@@ -448,10 +487,11 @@
         residual.reshape(fields),
         inverse_diagonal.reshape(V, V, 32, LANES),
         prior_increment.reshape(fields),
-        coupling.reshape(6, V * V),
+        coupling.transpose(1, 0, 2),
         characteristic.transpose(0, 3, 4, 1, 2).reshape(50, 2, 512),
         cutoffs,
-        jnp.asarray(table()),
+        jnp.asarray(high_low),
+        jnp.asarray(turns),
     )
     return result.reshape(V, GROUP, 8, LANES)
 

time: 35.8 us -> 34.5 us (0.964)
  the two profiles are of different devices: /device:TPU:2 before, /device:TPU:16 now
where the time goes in v2:
time: 34.5 us; the launch traced here: 34.3 us
  Pallas kernels  32.7 us (95%)
  local copies, waits for them, and re-layouts  1.53 us (4%)
    pallas_call x1, Pallas kernels, body(): pl.pallas_call(kernel, out_shape=jax.ShapeDtypeStruct(fields, f32), in_sp...  32.7 us
    unnamed x1, local copies, waits for them, and re-layouts  1.53 us

profile of v2, /device:TPU:16, one launch (start us, length us, event | category | flops | bytes accessed | tf_op | source)
XLA Modules:
  0.0 34.3 jit_solution(10669667313975561305)
XLA Ops:
  0.0 32.7 %shard_map.82 = f32[5,32,128]{2,1,0:T(8,128)} custom-call(f32[5,32,128]{2,1,0:T(8,128)} %bitcast.11, f32[5,5,32,128]{3,2,1,0:T(8,128)} %bitcast.8, f32[5,32,128]{2,1,0:T(8,128)} %bitcast.12, f32[5,6,5]{2,1,0:T(8,128)} %bitcast.13, f32[50,2,512]{2,1,0:T(2,128)} %bitcast.10, s32[2]{0:T(128)} %cutoffs.1, bf16[1856,128]{1,0:T(8,128)(2,1)} %constant.4.clone.const_in, ...), custom_call_target="tpu_custom_call" | custom-call | tf_op jit(solution)/shard_map/pallas_call | solution.py:479
  32.8 1.5 %copy.10 = f32[5,4,8,128]{3,2,1,0:T(8,128)} copy(f32[5,4,8,128]{3,2,1,0:T(8,128)} %bitcast.9) | data formatting | bytes 163840

commit v3 on v2

--- a/solution.py
+++ b/solution.py
@@ -101,13 +101,13 @@
 
 
 def kernel(
-    residual_in, inverse_in, prior_in, coupling, characteristic_in, cutoffs, const_in, turns_in, out,
-    residual, inverse, prior, characteristic, const, turns, load_s,
+    residual_in, inverse_in, prior_in, coupling_in, characteristic_in, cutoffs_in, const_in, turns_in, out,
+    residual, inverse, prior, coupling, cutoffs, characteristic, const, turns, load_s,
     lower, upper, edge_low, edge_high, planes_out, planes_in, corr_out, corr_in,
     maps_out, maps_in, layer_maps, vecs_out, vecs_in, layer_vecs, entry_out, entry_in,
-    down, up, first, second, third, source, base, flat, spectra,
+    down, up, first, second, third, next_reach, next_both, source, base, flat, spectra,
     pitch_s, pitch_r, back_s, back_r, side_s, side_r,
-    gm_s, gm_r, zm_s, zm_r, gv_s, gv_r, zv_s, zv_r, ge_s, ge_r,
+    gm_s, gm_r, zm_s, zm_r, zt_s, zt_r, gv_s, gv_r, zv_s, zv_r, ge_s, ge_r,
 ):
     pitch = lax.axis_index("pitch")
     span = lax.axis_index("span")
@@ -134,6 +134,7 @@
     for n, (src, dst) in enumerate((
         (residual_in, residual), (prior_in, prior), (inverse_in, inverse),
         (characteristic_in, characteristic), (const_in, const), (turns_in, turns),
+        (coupling_in, coupling), (cutoffs_in, cutoffs),
     )):
         loads.append(pltpu.make_async_copy(src, dst, load_s.at[n]))
         loads[-1].start()
@@ -178,6 +179,7 @@
     ]
 
     loads[2].wait()
+    loads[6].wait()
     reach = None
     for s in range(4):
         block = inverse[:, :, every(s, 4), :]
@@ -185,9 +187,6 @@
         up[s] = scaled(block, coupling, 1)
         reach = down[s] if s == 0 else product(down[s], reach)
         first[s] = reach
-    for k in range(V):
-        for i in range(V):
-            maps_out[every(8 * k + i, MAPS), :] = reach[k, i]
     both = reach
     trail = up[3]
     second[3] = both
@@ -197,8 +196,16 @@
         trail = product(up[s], trail)
         second[s] = both
         third[s] = trail
+    upper_reach = pltpu.roll(reach, 7, 2)
+    upper_both = pltpu.roll(both, 7, 2)
+    next_reach[...] = upper_reach
+    next_both[...] = upper_both
+    both = both + product(trail, product(upper_both, reach))
+    trail = product(trail, pltpu.roll(trail, 7, 2))
+    reach = product(upper_reach, reach)
     for k in range(V):
         for i in range(V):
+            maps_out[every(8 * k + i, MAPS), :] = reach[k, i]
             maps_out[every(40 + 8 * k + i, MAPS), :] = trail[k, i]
             maps_out[every(8 * k + 5 + i if i < 3 else 40 + 8 * k + 2 + i, MAPS), :] = both[k, i]
 
@@ -206,11 +213,11 @@
     for d in range(1, GROUP):
         to = lax.rem(member + d, GROUP)
         map_copies.append(send(
-            maps_out.at[rows(to * 2 * MAPS, 2 * MAPS)], maps_in.at[rows(member * 2 * MAPS, 2 * MAPS)],
+            maps_out.at[rows(to * 2 * MAPS, MAPS)], maps_in.at[rows(member * MAPS, MAPS)],
             gm_s.at[d], gm_r.at[d], at_member(d),
         ))
     planes_in[rows(pitch * LINE, LINE), :] = planes_out[rows(pitch * LINE, LINE), :]
-    maps_in[rows(member * 2 * MAPS, 2 * MAPS), :] = maps_out[rows(member * 2 * MAPS, 2 * MAPS), :]
+    maps_in[rows(member * MAPS, MAPS), :] = maps_out[rows(member * 2 * MAPS, MAPS), :]
 
     loads[3].wait()
     flat[100:104, :] = jnp.zeros((4, 512), jnp.float32)
@@ -233,8 +240,8 @@
 
     for copy in pitch_copies:
         copy.wait_recv()
-    loads[4].wait()
-    loads[5].wait()
+    for load in (loads[4], loads[5], loads[7]):
+        load.wait()
     spread = times(planes_in[...], const, SPREAD, 160, True).reshape(2, 10, 8, LANES)
     turn_re = turns[0:8, :][None]
     turn_im = turns[8:16, :][None]
@@ -297,12 +304,12 @@
     bottom = maps_in[40:80, :].reshape(V, 8, LANES)
     across = [moved(top, bottom)]
     forward = top
-    for n in range(1, 8):
+    for n in range(1, GROUP):
         parts = spread_rows(forward)
         forward = mix(tiles(maps_in, n, False), parts)
         across.append(moved(forward, mix(tiles(maps_in, n, True), parts)))
-    backward = jnp.concatenate([maps_in[7 * MAPS + 40 : 8 * MAPS, :].reshape(V, 8, LANES), across[7]], 0)
-    for n in range(6, -1, -1):
+    backward = jnp.concatenate([maps_in[3 * MAPS + 40 : 4 * MAPS, :].reshape(V, 8, LANES), across[3]], 0)
+    for n in range(GROUP - 2, -1, -1):
         backward = mix(tiles(maps_in, n, True), spread_rows(backward))
         backward = jnp.concatenate([backward[:V], backward[V:] + across[n]], 0)
     mine = pl.multiple_of(layer * MAPS, 8)
@@ -310,12 +317,19 @@
     whole_bottom = jnp.where(place < V, backward[:V], pltpu.roll(backward[V:], 2, 1))
     layer_maps[pl.ds(mine, 40), :] = whole_top.reshape(40, LANES)
     layer_maps[pl.ds(pl.multiple_of(layer * MAPS + 40, 8), 40), :] = whole_bottom.reshape(40, LANES)
-    layer_copies = []
+    layer_copies, lower_copies = [], []
     for d in range(1, LAYERS):
         layer_copies.append(send(
-            layer_maps.at[rows(layer * MAPS, MAPS)], layer_maps.at[rows(layer * MAPS, MAPS)],
+            layer_maps.at[rows(layer * MAPS, 40)], layer_maps.at[rows(layer * MAPS, 40)],
             zm_s.at[d], zm_r.at[d], at_layer(d),
         ))
+        copy = pltpu.make_async_remote_copy(
+            src_ref=layer_maps.at[rows(layer * MAPS + 40, 40)], dst_ref=layer_maps.at[rows(layer * MAPS + 40, 40)],
+            send_sem=zt_s.at[d], recv_sem=zt_r.at[d],
+            device_id=at_layer(d), device_id_type=pl.DeviceIdType.MESH,
+        )
+        lower_copies.append((copy, layer + d >= LAYERS, layer < d))
+        pl.when(layer + d >= LAYERS)(copy.start)
 
     for copy in side_copies:
         copy.wait_recv()
@@ -359,26 +373,27 @@
             value = value + block[:, j] * rhs[j][None]
         star = value if s == 0 else value + apply(down[s], star)
         base[s] = star
-    for i in range(V):
-        vecs_out[every(i, VECS), :] = star[i]
     update = star
     for s in (2, 1, 0):
         update = base[s] + apply(up[s], update)
         base[s] = update
+    ahead = pltpu.roll(star, 7, 1) + apply(next_reach, star)
+    behind = update + apply(third[0], pltpu.roll(update, 7, 1) + apply(next_both, star))
     for i in range(V):
-        vecs_out[every(8 + i, VECS), :] = update[i]
+        vecs_out[every(i, VECS), :] = ahead[i]
+        vecs_out[every(8 + i, VECS), :] = behind[i]
     vec_copies = []
     for d in range(1, GROUP):
         to = lax.rem(member + d, GROUP)
         vec_copies.append(send(
-            vecs_out.at[rows(to * 2 * VECS, 2 * VECS)], vecs_in.at[rows(member * 2 * VECS, 2 * VECS)],
+            vecs_out.at[rows(to * 2 * VECS, VECS)], vecs_in.at[rows(member * VECS, VECS)],
             gv_s.at[d], gv_r.at[d], at_member(d),
         ))
-    vecs_in[rows(member * 2 * VECS, 2 * VECS), :] = vecs_out[rows(member * 2 * VECS, 2 * VECS), :]
-
-    def chain(maps_ref, vecs_ref, x, y):
-        entering_x, entering_y, crossing = [], [None] * 8, []
-        for n in range(8):
+    vecs_in[rows(member * VECS, VECS), :] = vecs_out[rows(member * 2 * VECS, VECS), :]
+
+    def chain(count, maps_ref, vecs_ref, x, y):
+        entering_x, entering_y, crossing = [], [None] * count, []
+        for n in range(count):
             entering_x.append(x)
             offset = vecs_ref[n * VECS : n * VECS + 8, :]
             if x is None:
@@ -390,14 +405,14 @@
                 aside = mix(tiles(maps_ref, n, True), parts)
                 crossing.append(moved(ahead, aside) + vecs_ref[n * VECS + 8 : n * VECS + 16, :])
                 x = ahead + offset
-        for n in range(7, -1, -1):
+        for n in range(count - 1, -1, -1):
             entering_y[n] = y
             y = crossing[n] if y is None else mix(tiles(maps_ref, n, True), spread_rows(y)) + crossing[n]
         return entering_x, entering_y, x, y
 
     for copy in vec_copies:
         copy.wait_recv()
-    _, _, x, y = chain(maps_in, vecs_in, None, None)
+    _, _, x, y = chain(GROUP, maps_in, vecs_in, None, None)
     layer_vecs[pl.ds(pl.multiple_of(layer * VECS, 8), 8), :] = x
     layer_vecs[pl.ds(pl.multiple_of(layer * VECS + 8, 8), 8), :] = y
     vec_layer_copies = []
@@ -408,9 +423,11 @@
         ))
     for copy in layer_copies:
         copy.wait_recv()
+    for copy, _, comes in lower_copies:
+        pl.when(comes)(copy.wait_recv)
     for copy in vec_layer_copies:
         copy.wait_recv()
-    entering_x, entering_y, _, _ = chain(layer_maps, layer_vecs, None, None)
+    entering_x, entering_y, _, _ = chain(LAYERS, layer_maps, layer_vecs, None, None)
     x = jnp.zeros((8, LANES), jnp.float32)
     y = jnp.zeros((8, LANES), jnp.float32)
     for n in range(8):
@@ -418,10 +435,10 @@
             x = jnp.where(layer == n, entering_x[n], x)
         if entering_y[n] is not None:
             y = jnp.where(layer == n, entering_y[n], y)
-    entering_x, entering_y, _, _ = chain(maps_in, vecs_in, x, y)
+    entering_x, entering_y, _, _ = chain(GROUP, maps_in, vecs_in, x, y)
     for n in range(8):
-        entry_out[n * VECS : n * VECS + 8, :] = entering_x[n]
-        entry_out[n * VECS + 8 : n * VECS + 16, :] = entering_y[n]
+        entry_out[n * VECS : n * VECS + 8, :] = entering_x[n // 2]
+        entry_out[n * VECS + 8 : n * VECS + 16, :] = entering_y[n // 2]
     entry_copies = []
     for d in range(1, GROUP):
         to = lax.rem(member + d, GROUP)
@@ -432,8 +449,11 @@
     entry_in[rows(member * 2 * VECS, 2 * VECS), :] = entry_out[rows(member * 2 * VECS, 2 * VECS), :]
     for copy in entry_copies:
         copy.wait_recv()
-    x = [entry_in[every(i, VECS), :] for i in range(V)]
-    y = [entry_in[every(8 + i, VECS), :] for i in range(V)]
+    x = jnp.stack([entry_in[every(i, VECS), :] for i in range(V)])
+    y = jnp.stack([entry_in[every(8 + i, VECS), :] for i in range(V)])
+    odd = place % 2 == 1
+    x = jnp.where(odd, pltpu.roll(apply(first[3], x) + base[3], 1, 1), x)
+    y = jnp.where(odd, y, pltpu.roll(apply(third[0], y) + apply(second[0], x) + base[0], 7, 1))
     for s in range(4):
         value = base[s]
         for j in range(V):
@@ -445,6 +465,8 @@
         copy.wait_send()
     for copy in vec_copies + vec_layer_copies + entry_copies:
         copy.wait_send()
+    for copy, goes, _ in lower_copies:
+        pl.when(goes)(copy.wait_send)
 
 
 def body(residual, inverse_diagonal, prior_increment, coupling, characteristic, cutoffs):
@@ -460,26 +482,27 @@
 
     scratch = [
         pltpu.VMEM(fields, f32), pltpu.VMEM((V, V, 32, LANES), f32), pltpu.VMEM(fields, f32),
+        pltpu.SMEM((V, 6, V), f32), pltpu.SMEM((2,), jnp.int32),
         pltpu.VMEM((50, 2, 512), f32), pltpu.VMEM((2 * LOW, LANES), jnp.bfloat16), vmem(16),
-        pltpu.SemaphoreType.DMA((6,)),
+        pltpu.SemaphoreType.DMA((8,)),
         vmem(8), vmem(8), vmem(8), vmem(8),
         vmem(128), vmem(128), vmem(128), vmem(128),
         vmem(8 * MAPS), vmem(8 * MAPS), vmem(8 * MAPS),
         vmem(8 * VECS), vmem(8 * VECS), vmem(8 * VECS), vmem(8 * VECS), vmem(8 * VECS),
         matrices, matrices, matrices, matrices, matrices,
+        pltpu.VMEM((V, V, 8, LANES), f32), pltpu.VMEM((V, V, 8, LANES), f32),
         pltpu.VMEM(fields, f32), pltpu.VMEM((4, V, 8, LANES), f32),
         pltpu.VMEM((104, 512), f32), vmem(104 * 8),
         *sems(PITCH), *sems(PITCH), *sems(2),
-        *sems(GROUP), *sems(LAYERS), *sems(GROUP), *sems(LAYERS), *sems(GROUP),
+        *sems(GROUP), *sems(LAYERS), *sems(LAYERS), *sems(GROUP), *sems(LAYERS), *sems(GROUP),
     ]
     inside = pl.BlockSpec(memory_space=pltpu.VMEM)
     outside = pl.BlockSpec(memory_space=pl.ANY)
     high_low, turns = table()
-    scalars = pl.BlockSpec(memory_space=pltpu.SMEM)
     result = pl.pallas_call(
         kernel,
-        out_shape=jax.ShapeDtypeStruct(fields, f32),
-        in_specs=[outside, outside, outside, scalars, outside, scalars, outside, outside],
+        out_shape=pltpu.VMEM(fields, f32),
+        in_specs=[outside] * 8,
         out_specs=inside,
         scratch_shapes=scratch,
         compiler_params=pltpu.CompilerParams(collective_id=0, has_side_effects=True),

time: 34.5 us -> 30.3 us (0.88)
  the two profiles are of different devices: /device:TPU:16 before, /device:TPU:1 now
where the time goes in v3:
time: 30.3 us; the launch traced here: 30.2 us
  Pallas kernels  29.6 us (98%)
  local copies, waits for them, and re-layouts  0.64 us (2%)
    pallas_call x1, Pallas kernels, body(): pl.pallas_call(kernel, out_shape=pltpu.VMEM(fields, f32), in_specs=[outsi...  29.6 us
    unnamed x1, local copies, waits for them, and re-layouts  0.64 us

profile of v3, /device:TPU:1, one launch (start us, length us, event | category | flops | bytes accessed | tf_op | source)
XLA Modules:
  0.0 30.2 jit_solution(15270553228683217233)
XLA Ops:
  0.0 29.6 %shard_map.82 = f32[5,32,128]{2,1,0:T(8,128)S(1)} custom-call(f32[5,32,128]{2,1,0:T(8,128)} %bitcast.11, f32[5,5,32,128]{3,2,1,0:T(8,128)} %bitcast.9, f32[5,32,128]{2,1,0:T(8,128)} %bitcast.12, f32[5,6,5]{2,1,0:T(8,128)} %bitcast.13, f32[50,2,512]{2,1,0:T(2,128)} %bitcast.10, s32[2]{0:T(128)} %cutoffs_in.1, bf16[1856,128]{1,0:T(8,128)(2,1)} %constant.4.clone.const_in, ...), custom_call_target="tpu_custom_call" | custom-call | tf_op jit(solution)/shard_map/pallas_call | solution.py:502
  29.6 0.6 %copy.10 = f32[5,4,8,128]{3,2,1,0:T(8,128)} copy(f32[5,4,8,128]{3,2,1,0:T(8,128)S(1)} %bitcast.8) | data formatting | bytes 163840

commit v4 on v3

--- a/solution.py
+++ b/solution.py
@@ -13,7 +13,9 @@
 V = 5
 LINE = 16
 MAPS = 80
+A, B, C, USED = 0, 25, 50, 75
 VECS = 16
+SENT = 10
 LANES = 128
 
 SPREAD, FORWARD, BACK_RE, BACK_IM, GATHER_RE, GATHER_IM, LOW = np.cumsum([0, 160, 256, 128, 128, 128, 128]).tolist()
@@ -55,6 +57,10 @@
     return np.concatenate([high, low], 0), turns
 
 
+FAR_FIRST = (4, 3, 5, 2, 6, 1, 7)
+MEMBERS = (2, 1, 3)
+
+
 def every(start, stride):
     return pl.ds(start, 8, stride=stride)
 
@@ -104,10 +110,10 @@
     residual_in, inverse_in, prior_in, coupling_in, characteristic_in, cutoffs_in, const_in, turns_in, out,
     residual, inverse, prior, coupling, cutoffs, characteristic, const, turns, load_s,
     lower, upper, edge_low, edge_high, planes_out, planes_in, corr_out, corr_in,
-    maps_out, maps_in, layer_maps, vecs_out, vecs_in, layer_vecs, entry_out, entry_in,
+    maps_out, maps_in, packed, layer_maps, vecs_out, vecs_in, layer_vecs, entry_out, entry_in,
     down, up, first, second, third, next_reach, next_both, source, base, flat, spectra,
     pitch_s, pitch_r, back_s, back_r, side_s, side_r,
-    gm_s, gm_r, zm_s, zm_r, zt_s, zt_r, gv_s, gv_r, zv_s, zv_r, ge_s, ge_r,
+    gm_s, gm_r, gv_s, gv_r, zv_s, zv_r, ge_s, ge_r, zt_s, zt_r,
 ):
     pitch = lax.axis_index("pitch")
     span = lax.axis_index("span")
@@ -126,6 +132,8 @@
     peers = [at_pitch(d) for d in range(1, PITCH)]
     peers += [at_member(d) for d in range(1, GROUP)]
     peers += [at_layer(d) for d in range(1, LAYERS)]
+    for area in (planes_in, maps_in, layer_maps, vecs_in, layer_vecs, entry_in):
+        area[...] = jnp.zeros_like(area)
     barrier = pltpu.get_barrier_semaphore()
     for peer in peers:
         pl.semaphore_signal(barrier, inc=1, device_id=peer, device_id_type=pl.DeviceIdType.MESH)
@@ -145,7 +153,10 @@
             device_id=peer, device_id_type=pl.DeviceIdType.MESH,
         )
         copy.start()
-        return copy
+
+    def finish(sem, count):
+        area = maps_out.at[pl.ds(0, count)]
+        pltpu.make_async_copy(area, area, sem).wait()
 
     planes_out[...] = jnp.zeros_like(planes_out)
     maps_out[...] = jnp.zeros_like(maps_out)
@@ -157,13 +168,12 @@
 
     pl.semaphore_wait(barrier, len(peers))
 
-    pitch_copies = []
-    for d in range(1, PITCH):
+    for d in FAR_FIRST:
         to = lax.rem(pitch + d, PITCH)
-        pitch_copies.append(send(
-            planes_out.at[rows(to * LINE, LINE)], planes_in.at[rows(pitch * LINE, LINE)],
-            pitch_s.at[d], pitch_r.at[d], at_pitch(d),
-        ))
+        send(
+            planes_out.at[rows(to * LINE, SENT)], planes_in.at[rows(pitch * LINE, SENT)],
+            pitch_s, pitch_r, at_pitch(d),
+        )
     loads[1].wait()
     column = lax.broadcasted_iota(jnp.int32, (8, LANES), 1)
     last = initial = jnp.zeros((8, LANES), jnp.float32)
@@ -173,10 +183,8 @@
         initial = jnp.where(column == n, pltpu.roll(tile, n, 1) if n else tile, initial)
     edge_high[...] = last
     edge_low[...] = initial
-    side_copies = [
-        send(edge_high, lower, side_s.at[0], side_r.at[0], at_pitch(1)),
-        send(edge_low, upper, side_s.at[1], side_r.at[1], at_pitch(PITCH - 1)),
-    ]
+    send(edge_high, lower, side_s, side_r, at_pitch(1))
+    send(edge_low, upper, side_s, side_r, at_pitch(PITCH - 1))
 
     loads[2].wait()
     loads[6].wait()
@@ -205,17 +213,16 @@
     reach = product(upper_reach, reach)
     for k in range(V):
         for i in range(V):
-            maps_out[every(8 * k + i, MAPS), :] = reach[k, i]
-            maps_out[every(40 + 8 * k + i, MAPS), :] = trail[k, i]
-            maps_out[every(8 * k + 5 + i if i < 3 else 40 + 8 * k + 2 + i, MAPS), :] = both[k, i]
-
-    map_copies = []
-    for d in range(1, GROUP):
+            maps_out[every(A + V * k + i, MAPS), :] = reach[k, i]
+            maps_out[every(B + V * k + i, MAPS), :] = trail[k, i]
+            maps_out[every(C + V * k + i, MAPS), :] = both[k, i]
+
+    for d in MEMBERS:
         to = lax.rem(member + d, GROUP)
-        map_copies.append(send(
-            maps_out.at[rows(to * 2 * MAPS, MAPS)], maps_in.at[rows(member * MAPS, MAPS)],
-            gm_s.at[d], gm_r.at[d], at_member(d),
-        ))
+        send(
+            maps_out.at[rows(to * 2 * MAPS, USED)], maps_in.at[rows(member * MAPS, USED)],
+            gm_s, gm_r, at_member(d),
+        )
     planes_in[rows(pitch * LINE, LINE), :] = planes_out[rows(pitch * LINE, LINE), :]
     maps_in[rows(member * MAPS, MAPS), :] = maps_out[rows(member * 2 * MAPS, MAPS), :]
 
@@ -238,8 +245,7 @@
         part = part + jnp.dot(low, pick, preferred_element_type=jnp.float32)
         spectra[pl.ds(k1, 104, stride=8), :] = part
 
-    for copy in pitch_copies:
-        copy.wait_recv()
+    finish(pitch_r, (PITCH - 1) * SENT)
     for load in (loads[4], loads[5], loads[7]):
         load.wait()
     spread = times(planes_in[...], const, SPREAD, 160, True).reshape(2, 10, 8, LANES)
@@ -270,20 +276,19 @@
     lines_re = jnp.concatenate([(back_re * turn_re - back_im * turn_im).reshape(80, LANES), filler], 0)
     lines_im = jnp.concatenate([(back_im * turn_re + back_re * turn_im).reshape(80, LANES), filler], 0)
     corr_out[...] = times(lines_re, const, GATHER_RE, 128, True) + times(lines_im, const, GATHER_IM, 128, True)
-    back_copies = []
-    for d in range(1, PITCH):
+    for d in FAR_FIRST:
         to = lax.rem(pitch + d, PITCH)
-        back_copies.append(send(
-            corr_out.at[rows(to * LINE, LINE)], corr_in.at[rows(pitch * LINE, LINE)],
-            back_s.at[d], back_r.at[d], at_pitch(d),
-        ))
+        send(
+            corr_out.at[rows(to * LINE, SENT)], corr_in.at[rows(pitch * LINE, SENT)],
+            back_s, back_r, at_pitch(d),
+        )
     corr_in[rows(pitch * LINE, LINE), :] = corr_out[rows(pitch * LINE, LINE), :]
 
     place = lax.broadcasted_iota(jnp.int32, (8, LANES), 0)
 
-    def tiles(ref, n, second_half):
-        start = n * MAPS + (40 if second_half else 0)
-        return [ref[start + 8 * j : start + 8 * j + 8, :] for j in range(V)]
+    def tiles(ref, n, which):
+        start = n * MAPS + which
+        return [ref[start + V * j : start + V * j + 8, :] for j in range(V)]
 
     def spread_rows(vector):
         return [jnp.broadcast_to(vector[..., j : j + 1, :], vector.shape) for j in range(V)]
@@ -294,45 +299,36 @@
             total = total + matrix[j] * parts[j]
         return total
 
-    def moved(top, bottom):
-        axis = top.ndim - 2
-        return jnp.where(place < 3, pltpu.roll(top, 3, axis), pltpu.roll(bottom, 6, axis))
-
-    for copy in map_copies:
-        copy.wait_recv()
-    top = maps_in[0:40, :].reshape(V, 8, LANES)
-    bottom = maps_in[40:80, :].reshape(V, 8, LANES)
-    across = [moved(top, bottom)]
-    forward = top
+    finish(gm_r, (GROUP - 1) * USED)
+    forward = jnp.stack(tiles(maps_in, 0, A))
+    across = [jnp.stack(tiles(maps_in, 0, C))]
     for n in range(1, GROUP):
         parts = spread_rows(forward)
-        forward = mix(tiles(maps_in, n, False), parts)
-        across.append(moved(forward, mix(tiles(maps_in, n, True), parts)))
-    backward = jnp.concatenate([maps_in[3 * MAPS + 40 : 4 * MAPS, :].reshape(V, 8, LANES), across[3]], 0)
+        forward = mix(tiles(maps_in, n, A), parts)
+        across.append(mix(tiles(maps_in, n, C), parts))
+    backward = jnp.concatenate([jnp.stack(tiles(maps_in, GROUP - 1, B)), across[GROUP - 1]], 0)
     for n in range(GROUP - 2, -1, -1):
-        backward = mix(tiles(maps_in, n, True), spread_rows(backward))
+        backward = mix(tiles(maps_in, n, B), spread_rows(backward))
         backward = jnp.concatenate([backward[:V], backward[V:] + across[n]], 0)
-    mine = pl.multiple_of(layer * MAPS, 8)
-    whole_top = jnp.where(place < V, forward, pltpu.roll(backward[V:], 5, 1))
-    whole_bottom = jnp.where(place < V, backward[:V], pltpu.roll(backward[V:], 2, 1))
-    layer_maps[pl.ds(mine, 40), :] = whole_top.reshape(40, LANES)
-    layer_maps[pl.ds(pl.multiple_of(layer * MAPS + 40, 8), 40), :] = whole_bottom.reshape(40, LANES)
-    layer_copies, lower_copies = [], []
-    for d in range(1, LAYERS):
-        layer_copies.append(send(
-            layer_maps.at[rows(layer * MAPS, 40)], layer_maps.at[rows(layer * MAPS, 40)],
-            zm_s.at[d], zm_r.at[d], at_layer(d),
-        ))
-        copy = pltpu.make_async_remote_copy(
-            src_ref=layer_maps.at[rows(layer * MAPS + 40, 40)], dst_ref=layer_maps.at[rows(layer * MAPS + 40, 40)],
-            send_sem=zt_s.at[d], recv_sem=zt_r.at[d],
-            device_id=at_layer(d), device_id_type=pl.DeviceIdType.MESH,
-        )
-        lower_copies.append((copy, layer + d >= LAYERS, layer < d))
-        pl.when(layer + d >= LAYERS)(copy.start)
-
-    for copy in side_copies:
-        copy.wait_recv()
+    columns = jnp.concatenate([forward, backward], 0)
+    for n in range(3 * V):
+        packed[V * n : V * n + 8, :] = columns[n]
+    layer_maps[rows(layer * MAPS, MAPS), :] = packed[0:MAPS, :]
+    lower_copies = []
+    for d in FAR_FIRST:
+        wraps = layer + d >= LAYERS
+        pieces = []
+        for size, n in ((USED, d - 1), (B, LAYERS - 2 + d)):
+            pieces.append(pltpu.make_async_remote_copy(
+                src_ref=layer_maps.at[rows(layer * MAPS, size)], dst_ref=layer_maps.at[rows(layer * MAPS, size)],
+                send_sem=zt_s.at[n], recv_sem=zt_r.at[n],
+                device_id=at_layer(d), device_id_type=pl.DeviceIdType.MESH,
+            ))
+        lower_copies.append((pieces, wraps, layer < d))
+        pl.when(wraps)(pieces[0].start)
+        pl.when(jnp.logical_not(wraps))(pieces[1].start)
+
+    finish(side_r, 16)
     own = prior[...]
     below, above = [], []
     for i in range(V):
@@ -359,8 +355,7 @@
         total = total - jnp.concatenate([zero_row, before[:24]], 0) - jnp.concatenate([after[8:], zero_row], 0)
         source[i] = total
 
-    for copy in back_copies:
-        copy.wait_recv()
+    finish(back_r, (PITCH - 1) * SENT)
     for j in range(V):
         source[j, 0:8, :] = source[j, 0:8, :] + corr_in[every(j, LINE), :]
         source[j, 24:32, :] = source[j, 24:32, :] + corr_in[every(V + j, LINE), :]
@@ -381,14 +376,13 @@
     behind = update + apply(third[0], pltpu.roll(update, 7, 1) + apply(next_both, star))
     for i in range(V):
         vecs_out[every(i, VECS), :] = ahead[i]
-        vecs_out[every(8 + i, VECS), :] = behind[i]
-    vec_copies = []
-    for d in range(1, GROUP):
+        vecs_out[every(V + i, VECS), :] = behind[i]
+    for d in MEMBERS:
         to = lax.rem(member + d, GROUP)
-        vec_copies.append(send(
-            vecs_out.at[rows(to * 2 * VECS, VECS)], vecs_in.at[rows(member * VECS, VECS)],
-            gv_s.at[d], gv_r.at[d], at_member(d),
-        ))
+        send(
+            vecs_out.at[rows(to * 2 * VECS, SENT)], vecs_in.at[rows(member * VECS, SENT)],
+            gv_s, gv_r, at_member(d),
+        )
     vecs_in[rows(member * VECS, VECS), :] = vecs_out[rows(member * 2 * VECS, VECS), :]
 
     def chain(count, maps_ref, vecs_ref, x, y):
@@ -397,36 +391,32 @@
             entering_x.append(x)
             offset = vecs_ref[n * VECS : n * VECS + 8, :]
             if x is None:
-                crossing.append(vecs_ref[n * VECS + 8 : n * VECS + 16, :])
+                crossing.append(vecs_ref[n * VECS + V : n * VECS + V + 8, :])
                 x = offset
             else:
                 parts = spread_rows(x)
-                ahead = mix(tiles(maps_ref, n, False), parts)
-                aside = mix(tiles(maps_ref, n, True), parts)
-                crossing.append(moved(ahead, aside) + vecs_ref[n * VECS + 8 : n * VECS + 16, :])
+                ahead = mix(tiles(maps_ref, n, A), parts)
+                crossing.append(mix(tiles(maps_ref, n, C), parts) + vecs_ref[n * VECS + V : n * VECS + V + 8, :])
                 x = ahead + offset
         for n in range(count - 1, -1, -1):
             entering_y[n] = y
-            y = crossing[n] if y is None else mix(tiles(maps_ref, n, True), spread_rows(y)) + crossing[n]
+            y = crossing[n] if y is None else mix(tiles(maps_ref, n, B), spread_rows(y)) + crossing[n]
         return entering_x, entering_y, x, y
 
-    for copy in vec_copies:
-        copy.wait_recv()
+    finish(gv_r, (GROUP - 1) * SENT)
     _, _, x, y = chain(GROUP, maps_in, vecs_in, None, None)
-    layer_vecs[pl.ds(pl.multiple_of(layer * VECS, 8), 8), :] = x
-    layer_vecs[pl.ds(pl.multiple_of(layer * VECS + 8, 8), 8), :] = y
-    vec_layer_copies = []
-    for d in range(1, LAYERS):
-        vec_layer_copies.append(send(
-            layer_vecs.at[rows(layer * VECS, VECS)], layer_vecs.at[rows(layer * VECS, VECS)],
-            zv_s.at[d], zv_r.at[d], at_layer(d),
-        ))
-    for copy in layer_copies:
-        copy.wait_recv()
-    for copy, _, comes in lower_copies:
-        pl.when(comes)(copy.wait_recv)
-    for copy in vec_layer_copies:
-        copy.wait_recv()
+    tail = pltpu.roll(y, V, 0)
+    layer_vecs[rows(layer * VECS, 8), :] = jnp.where(place < V, x, tail)
+    layer_vecs[rows(layer * VECS + 8, 8), :] = tail
+    for d in FAR_FIRST:
+        send(
+            layer_vecs.at[rows(layer * VECS, SENT)], layer_vecs.at[rows(layer * VECS, SENT)],
+            zv_s, zv_r, at_layer(d),
+        )
+    for pieces, _, from_above in lower_copies:
+        pl.when(from_above)(pieces[0].wait_recv)
+        pl.when(jnp.logical_not(from_above))(pieces[1].wait_recv)
+    finish(zv_r, (LAYERS - 1) * SENT)
     entering_x, entering_y, _, _ = chain(LAYERS, layer_maps, layer_vecs, None, None)
     x = jnp.zeros((8, LANES), jnp.float32)
     y = jnp.zeros((8, LANES), jnp.float32)
@@ -436,23 +426,23 @@
         if entering_y[n] is not None:
             y = jnp.where(layer == n, entering_y[n], y)
     entering_x, entering_y, _, _ = chain(GROUP, maps_in, vecs_in, x, y)
-    for n in range(8):
-        entry_out[n * VECS : n * VECS + 8, :] = entering_x[n // 2]
-        entry_out[n * VECS + 8 : n * VECS + 16, :] = entering_y[n // 2]
-    entry_copies = []
-    for d in range(1, GROUP):
+    for n in range(GROUP):
+        tail = pltpu.roll(entering_y[n], V, 0)
+        entry_out[n * VECS : n * VECS + 8, :] = jnp.where(place < V, entering_x[n], tail)
+        entry_out[n * VECS + 8 : n * VECS + 16, :] = tail
+    for d in MEMBERS:
         to = lax.rem(member + d, GROUP)
-        entry_copies.append(send(
-            entry_out.at[rows(to * 2 * VECS, 2 * VECS)], entry_in.at[rows(member * 2 * VECS, 2 * VECS)],
-            ge_s.at[d], ge_r.at[d], at_member(d),
-        ))
-    entry_in[rows(member * 2 * VECS, 2 * VECS), :] = entry_out[rows(member * 2 * VECS, 2 * VECS), :]
-    for copy in entry_copies:
-        copy.wait_recv()
+        send(
+            entry_out.at[rows(to * VECS, SENT)], entry_in.at[rows(member * 2 * VECS, SENT)],
+            ge_s, ge_r, at_member(d),
+        )
+    entry_in[rows(member * 2 * VECS, VECS), :] = entry_out[rows(member * VECS, VECS), :]
+    finish(ge_r, (GROUP - 1) * SENT)
     x = jnp.stack([entry_in[every(i, VECS), :] for i in range(V)])
-    y = jnp.stack([entry_in[every(8 + i, VECS), :] for i in range(V)])
+    y = jnp.stack([entry_in[every(V + i, VECS), :] for i in range(V)])
     odd = place % 2 == 1
     x = jnp.where(odd, pltpu.roll(apply(first[3], x) + base[3], 1, 1), x)
+    y = jnp.where(odd, pltpu.roll(y, 1, 1), y)
     y = jnp.where(odd, y, pltpu.roll(apply(third[0], y) + apply(second[0], x) + base[0], 7, 1))
     for s in range(4):
         value = base[s]
@@ -461,12 +451,16 @@
         for i in range(V):
             out[i, every(s, 4), :] = value[i]
 
-    for copy in pitch_copies + side_copies + map_copies + back_copies + layer_copies:
-        copy.wait_send()
-    for copy in vec_copies + vec_layer_copies + entry_copies:
-        copy.wait_send()
-    for copy, goes, _ in lower_copies:
-        pl.when(goes)(copy.wait_send)
+    finish(pitch_s, (PITCH - 1) * SENT)
+    finish(side_s, 16)
+    finish(gm_s, (GROUP - 1) * USED)
+    finish(back_s, (PITCH - 1) * SENT)
+    finish(gv_s, (GROUP - 1) * SENT)
+    finish(zv_s, (LAYERS - 1) * SENT)
+    finish(ge_s, (GROUP - 1) * SENT)
+    for pieces, wraps, _ in lower_copies:
+        pl.when(wraps)(pieces[0].wait_send)
+        pl.when(jnp.logical_not(wraps))(pieces[1].wait_send)
 
 
 def body(residual, inverse_diagonal, prior_increment, coupling, characteristic, cutoffs):
@@ -476,9 +470,6 @@
 
     def vmem(count):
         return pltpu.VMEM((count, LANES), f32)
-
-    def sems(count):
-        return [pltpu.SemaphoreType.DMA((count,))] * 2
 
     scratch = [
         pltpu.VMEM(fields, f32), pltpu.VMEM((V, V, 32, LANES), f32), pltpu.VMEM(fields, f32),
@@ -487,14 +478,13 @@
         pltpu.SemaphoreType.DMA((8,)),
         vmem(8), vmem(8), vmem(8), vmem(8),
         vmem(128), vmem(128), vmem(128), vmem(128),
-        vmem(8 * MAPS), vmem(8 * MAPS), vmem(8 * MAPS),
-        vmem(8 * VECS), vmem(8 * VECS), vmem(8 * VECS), vmem(8 * VECS), vmem(8 * VECS),
+        vmem(8 * MAPS), vmem(GROUP * MAPS), vmem(MAPS), vmem(LAYERS * MAPS),
+        vmem(8 * VECS), vmem(GROUP * VECS), vmem(LAYERS * VECS), vmem(GROUP * VECS), vmem(8 * VECS),
         matrices, matrices, matrices, matrices, matrices,
         pltpu.VMEM((V, V, 8, LANES), f32), pltpu.VMEM((V, V, 8, LANES), f32),
         pltpu.VMEM(fields, f32), pltpu.VMEM((4, V, 8, LANES), f32),
         pltpu.VMEM((104, 512), f32), vmem(104 * 8),
-        *sems(PITCH), *sems(PITCH), *sems(2),
-        *sems(GROUP), *sems(LAYERS), *sems(LAYERS), *sems(GROUP), *sems(LAYERS), *sems(GROUP),
+        *[pltpu.SemaphoreType.DMA] * 14, *[pltpu.SemaphoreType.DMA((2 * (LAYERS - 1),))] * 2,
     ]
     inside = pl.BlockSpec(memory_space=pltpu.VMEM)
     outside = pl.BlockSpec(memory_space=pl.ANY)

time: 30.3 us -> 28.7 us (0.947)
  the two profiles are of different devices: /device:TPU:1 before, /device:TPU:2 now
where the time goes in v4:
time: 28.7 us; the launch traced here: 28.2 us
  Pallas kernels  27.6 us (96%)
  local copies, waits for them, and re-layouts  0.64 us (2%)
    pallas_call x1, Pallas kernels, body(): pl.pallas_call(kernel, out_shape=pltpu.VMEM(fields, f32), in_specs=[outsi...  27.6 us
    unnamed x1, local copies, waits for them, and re-layouts  0.64 us

profile of v4, /device:TPU:2, one launch (start us, length us, event | category | flops | bytes accessed | tf_op | source)
XLA Modules:
  0.0 28.2 jit_solution(9791821090042257994)
XLA Ops:
  0.0 27.6 %shard_map.82 = f32[5,32,128]{2,1,0:T(8,128)S(1)} custom-call(f32[5,32,128]{2,1,0:T(8,128)} %bitcast.11, f32[5,5,32,128]{3,2,1,0:T(8,128)} %bitcast.9, f32[5,32,128]{2,1,0:T(8,128)} %bitcast.12, f32[5,6,5]{2,1,0:T(8,128)} %bitcast.13, f32[50,2,512]{2,1,0:T(2,128)} %bitcast.10, s32[2]{0:T(128)} %cutoffs_in.1, bf16[1856,128]{1,0:T(8,128)(2,1)} %constant.4.clone.const_in, ...), custom_call_target="tpu_custom_call" | custom-call | tf_op jit(solution)/shard_map/pallas_call | solution.py:492
  27.6 0.6 %copy.10 = f32[5,4,8,128]{3,2,1,0:T(8,128)} copy(f32[5,4,8,128]{3,2,1,0:T(8,128)S(1)} %bitcast.8) | data formatting | bytes 163840

commit v5 on v4

--- a/solution.py
+++ b/solution.py
@@ -12,13 +12,15 @@
 LAYERS = 8
 V = 5
 LINE = 16
-MAPS = 80
-A, B, C, USED = 0, 25, 50, 75
+MAPS = 88
+B, C, A = 0, 25, 56
+PAIR, SINGLE, USED = 50, 25, 81
 VECS = 16
 SENT = 10
 LANES = 128
 
-SPREAD, FORWARD, BACK_RE, BACK_IM, GATHER_RE, GATHER_IM, LOW = np.cumsum([0, 160, 256, 128, 128, 128, 128]).tolist()
+FORWARD, BACK_RE, BACK_IM, LOW = 0, 256, 384, 512
+HALF = float(np.sqrt(0.5))
 
 
 def table():
@@ -26,30 +28,13 @@
     a = np.arange(8)
     b = np.arange(128)
     k2 = np.arange(64)
-    eight = two_pi * (np.outer(a, a) % 8) / 8
-    spread = np.zeros((2, 10, 8, 8, LINE))
-    for line in range(10):
-        spread[0, line, :, :, line] = np.cos(eight)
-        spread[1, line, :, :, line] = -np.sin(eight)
     twiddle = two_pi * np.outer(a, b) / NP
     lanes = two_pi * (np.outer(b, k2) % 128) / 128
     cos, sin = np.cos(lanes), np.sin(lanes)
     forward = np.block([[cos, -sin], [sin, cos]])
     back_re = np.concatenate([cos.T, -sin.T], 0)
     back_im = np.concatenate([sin.T, cos.T], 0)
-    gather_re = np.zeros((8, LINE, 16, 8))
-    gather_im = np.zeros((8, LINE, 16, 8))
-    for line in range(10):
-        gather_re[:, line, line, :] = np.cos(eight)
-        gather_im[:, line, line, :] = -np.sin(eight)
-    parts = [
-        spread.reshape(160, 128),
-        forward,
-        back_re,
-        back_im,
-        gather_re.reshape(128, 128),
-        gather_im.reshape(128, 128),
-    ]
+    parts = [forward, back_re, back_im]
     whole = np.concatenate(parts, 0).astype(np.float32)
     high = whole.astype(jnp.bfloat16)
     low = (whole - high.astype(np.float32)).astype(jnp.bfloat16)
@@ -93,27 +78,51 @@
     return jnp.stack(columns)
 
 
-def times(data, const, start, size, left=False):
+def times(data, const, start, size):
     data_high = data.astype(jnp.bfloat16)
     data_low = (data - data_high.astype(jnp.float32)).astype(jnp.bfloat16)
     high = const[start : start + size, :]
     low = const[LOW + start : LOW + start + size, :]
-    pairs = ((data_high, high), (data_low, high), (data_high, low))
-    total = None
-    for x, w in pairs:
-        part = jnp.dot(w, x, preferred_element_type=jnp.float32) if left else jnp.dot(x, w, preferred_element_type=jnp.float32)
-        total = part if total is None else total + part
-    return total
+    total = jnp.dot(data_high, high, preferred_element_type=jnp.float32)
+    total = total + jnp.dot(data_low, high, preferred_element_type=jnp.float32)
+    return total + jnp.dot(data_high, low, preferred_element_type=jnp.float32)
+
+
+def eight_forward(x):
+    s0, d0, s2, d2 = x[0] + x[4], x[0] - x[4], x[2] + x[6], x[2] - x[6]
+    s1, d1, s3, d3 = x[1] + x[5], x[1] - x[5], x[3] + x[7], x[3] - x[7]
+    even, odd = s0 + s2, s1 + s3
+    real, imag = s0 - s2, s3 - s1
+    near, far = HALF * (d1 - d3), HALF * (d1 + d3)
+    zero = jnp.zeros_like(even)
+    first = (d0 + near, -(d2 + far))
+    third = (d0 - near, d2 - far)
+    return [
+        (even + odd, zero), first, (real, imag), third,
+        (even - odd, zero), (third[0], -third[1]), (real, -imag), (first[0], -first[1]),
+    ]
+
+
+def eight_back(re, im):
+    p1, p2, p3 = re[1] + re[7], re[2] + re[6], re[3] + re[5]
+    q1, q2, q3 = im[1] - im[7], im[2] - im[6], im[3] - im[5]
+    total, gap = re[0] + re[4], re[0] - re[4]
+    both, part = p1 + p3, HALF * (p1 - p3)
+    cross, lean = q1 - q3, HALF * (q1 + q3)
+    return [
+        total + p2 + both, gap - q2 + part - lean, total - p2 - cross, gap + q2 - part - lean,
+        total + p2 - both, gap - q2 - part + lean, total - p2 + cross, gap + q2 + part + lean,
+    ]
 
 
 def kernel(
     residual_in, inverse_in, prior_in, coupling_in, characteristic_in, cutoffs_in, const_in, turns_in, out,
     residual, inverse, prior, coupling, cutoffs, characteristic, const, turns, load_s,
-    lower, upper, edge_low, edge_high, planes_out, planes_in, corr_out, corr_in,
+    lower, upper, edge_low, edge_high, planes_out, planes_in, ordered, corr_out, corr_in,
     maps_out, maps_in, packed, layer_maps, vecs_out, vecs_in, layer_vecs, entry_out, entry_in,
     down, up, first, second, third, next_reach, next_both, source, base, flat, spectra,
     pitch_s, pitch_r, back_s, back_r, side_s, side_r,
-    gm_s, gm_r, gv_s, gv_r, zv_s, zv_r, ge_s, ge_r, zt_s, zt_r,
+    gm_s, gm_r, zm_s, zm_r, gv_s, gv_r, zv_s, zv_r, ge_s, ge_r, zt_s, zt_r,
 ):
     pitch = lax.axis_index("pitch")
     span = lax.axis_index("span")
@@ -132,6 +141,7 @@
     peers = [at_pitch(d) for d in range(1, PITCH)]
     peers += [at_member(d) for d in range(1, GROUP)]
     peers += [at_layer(d) for d in range(1, LAYERS)]
+    packed[...] = jnp.zeros_like(packed)
     for area in (planes_in, maps_in, layer_maps, vecs_in, layer_vecs, entry_in):
         area[...] = jnp.zeros_like(area)
     barrier = pltpu.get_barrier_semaphore()
@@ -248,18 +258,20 @@
     finish(pitch_r, (PITCH - 1) * SENT)
     for load in (loads[4], loads[5], loads[7]):
         load.wait()
-    spread = times(planes_in[...], const, SPREAD, 160, True).reshape(2, 10, 8, LANES)
-    turn_re = turns[0:8, :][None]
-    turn_im = turns[8:16, :][None]
-    turned_re = (spread[0] * turn_re + spread[1] * turn_im).reshape(80, LANES)
-    turned_im = (spread[1] * turn_re - spread[0] * turn_im).reshape(80, LANES)
-    spectrum = times(jnp.concatenate([turned_re, turned_im], 1), const, FORWARD, 256)
+    turned_re, turned_im = [], []
+    parts = eight_forward([planes_in[a * LINE : a * LINE + LINE, :] for a in range(8)])
+    for k1, (re, im) in enumerate(parts):
+        turn_re, turn_im = turns[k1 : k1 + 1, :], turns[8 + k1 : 9 + k1, :]
+        turned_re.append(re * turn_re + im * turn_im)
+        turned_im.append(im * turn_re - re * turn_im)
+    turned = jnp.concatenate([jnp.concatenate(turned_re, 0), jnp.concatenate(turned_im, 0)], 1)
+    ordered[...] = times(turned, const, FORWARD, 256)
+    spectrum = jnp.concatenate([ordered[every(line, LINE), :] for line in range(2 * V)], 0)
     number = lax.broadcasted_iota(jnp.int32, (8, LANES), 0) + 8 * (lax.broadcasted_iota(jnp.int32, (8, LANES), 1) % 64)
     weight = jnp.where(number == 0, 1.0, 2.0) / NP
     sign = jnp.where(lax.broadcasted_iota(jnp.int32, (80, LANES), 1) < 64, -1.0, 1.0)
     crossed = (pltpu.roll(spectrum, 64, 1) * sign).reshape(2, V, 8, LANES)
     spectrum = spectrum.reshape(2, V, 8, LANES)
-    corrected = []
     for q in range(2):
         factor = jnp.where(number < cutoffs[q], weight, 0.0)
         for i in range(V):
@@ -268,14 +280,18 @@
                 row = (q * 25 + i * V + j) * 16
                 term = spectra[row : row + 8, :] * spectrum[q, j] + spectra[row + 8 : row + 16, :] * crossed[q, j]
                 total = term if total is None else total + term
-            corrected.append(total * factor)
-    corrected = jnp.concatenate(corrected, 0)
-    back_re = times(corrected, const, BACK_RE, 128).reshape(10, 8, LANES)
-    back_im = times(corrected, const, BACK_IM, 128).reshape(10, 8, LANES)
-    filler = jnp.zeros((48, LANES), jnp.float32)
-    lines_re = jnp.concatenate([(back_re * turn_re - back_im * turn_im).reshape(80, LANES), filler], 0)
-    lines_im = jnp.concatenate([(back_im * turn_re + back_re * turn_im).reshape(80, LANES), filler], 0)
-    corr_out[...] = times(lines_re, const, GATHER_RE, 128, True) + times(lines_im, const, GATHER_IM, 128, True)
+            ordered[every(q * V + i, LINE), :] = total * factor
+    corrected = ordered[...]
+    back_re = times(corrected, const, BACK_RE, 128)
+    back_im = times(corrected, const, BACK_IM, 128)
+    lines_re, lines_im = [], []
+    for k1 in range(8):
+        turn_re, turn_im = turns[k1 : k1 + 1, :], turns[8 + k1 : 9 + k1, :]
+        re, im = back_re[k1 * LINE : k1 * LINE + LINE], back_im[k1 * LINE : k1 * LINE + LINE]
+        lines_re.append(re * turn_re - im * turn_im)
+        lines_im.append(im * turn_re + re * turn_im)
+    for a, value in enumerate(eight_back(lines_re, lines_im)):
+        corr_out[a * LINE : a * LINE + LINE, :] = value
     for d in FAR_FIRST:
         to = lax.rem(pitch + d, PITCH)
         send(
@@ -312,21 +328,22 @@
         backward = jnp.concatenate([backward[:V], backward[V:] + across[n]], 0)
     columns = jnp.concatenate([forward, backward], 0)
     for n in range(3 * V):
-        packed[V * n : V * n + 8, :] = columns[n]
-    layer_maps[rows(layer * MAPS, MAPS), :] = packed[0:MAPS, :]
+        start = A + V * n if n < V else V * n - 25
+        packed[start : start + 8, :] = columns[n]
+    layer_maps[rows(layer * MAPS, MAPS), :] = packed[...]
     lower_copies = []
     for d in FAR_FIRST:
-        wraps = layer + d >= LAYERS
-        pieces = []
-        for size, n in ((USED, d - 1), (B, LAYERS - 2 + d)):
-            pieces.append(pltpu.make_async_remote_copy(
-                src_ref=layer_maps.at[rows(layer * MAPS, size)], dst_ref=layer_maps.at[rows(layer * MAPS, size)],
-                send_sem=zt_s.at[n], recv_sem=zt_r.at[n],
-                device_id=at_layer(d), device_id_type=pl.DeviceIdType.MESH,
-            ))
-        lower_copies.append((pieces, wraps, layer < d))
-        pl.when(wraps)(pieces[0].start)
-        pl.when(jnp.logical_not(wraps))(pieces[1].start)
+        send(
+            layer_maps.at[rows(layer * MAPS + A, SINGLE)], layer_maps.at[rows(layer * MAPS + A, SINGLE)],
+            zm_s, zm_r, at_layer(d),
+        )
+        copy = pltpu.make_async_remote_copy(
+            src_ref=layer_maps.at[rows(layer * MAPS, PAIR)], dst_ref=layer_maps.at[rows(layer * MAPS, PAIR)],
+            send_sem=zt_s.at[d - 1], recv_sem=zt_r.at[d - 1],
+            device_id=at_layer(d), device_id_type=pl.DeviceIdType.MESH,
+        )
+        lower_copies.append((copy, layer + d >= LAYERS, layer < d))
+        pl.when(layer + d >= LAYERS)(copy.start)
 
     finish(side_r, 16)
     own = prior[...]
@@ -413,9 +430,9 @@
             layer_vecs.at[rows(layer * VECS, SENT)], layer_vecs.at[rows(layer * VECS, SENT)],
             zv_s, zv_r, at_layer(d),
         )
-    for pieces, _, from_above in lower_copies:
-        pl.when(from_above)(pieces[0].wait_recv)
-        pl.when(jnp.logical_not(from_above))(pieces[1].wait_recv)
+    finish(zm_r, (LAYERS - 1) * SINGLE)
+    for copy, _, from_above in lower_copies:
+        pl.when(from_above)(copy.wait_recv)
     finish(zv_r, (LAYERS - 1) * SENT)
     entering_x, entering_y, _, _ = chain(LAYERS, layer_maps, layer_vecs, None, None)
     x = jnp.zeros((8, LANES), jnp.float32)
@@ -458,9 +475,9 @@
     finish(gv_s, (GROUP - 1) * SENT)
     finish(zv_s, (LAYERS - 1) * SENT)
     finish(ge_s, (GROUP - 1) * SENT)
-    for pieces, wraps, _ in lower_copies:
-        pl.when(wraps)(pieces[0].wait_send)
-        pl.when(jnp.logical_not(wraps))(pieces[1].wait_send)
+    finish(zm_s, (LAYERS - 1) * SINGLE)
+    for copy, wraps, _ in lower_copies:
+        pl.when(wraps)(copy.wait_send)
 
 
 def body(residual, inverse_diagonal, prior_increment, coupling, characteristic, cutoffs):
@@ -477,14 +494,14 @@
         pltpu.VMEM((50, 2, 512), f32), pltpu.VMEM((2 * LOW, LANES), jnp.bfloat16), vmem(16),
         pltpu.SemaphoreType.DMA((8,)),
         vmem(8), vmem(8), vmem(8), vmem(8),
-        vmem(128), vmem(128), vmem(128), vmem(128),
+        vmem(128), vmem(128), vmem(128), vmem(128), vmem(128),
         vmem(8 * MAPS), vmem(GROUP * MAPS), vmem(MAPS), vmem(LAYERS * MAPS),
         vmem(8 * VECS), vmem(GROUP * VECS), vmem(LAYERS * VECS), vmem(GROUP * VECS), vmem(8 * VECS),
         matrices, matrices, matrices, matrices, matrices,
         pltpu.VMEM((V, V, 8, LANES), f32), pltpu.VMEM((V, V, 8, LANES), f32),
         pltpu.VMEM(fields, f32), pltpu.VMEM((4, V, 8, LANES), f32),
         pltpu.VMEM((104, 512), f32), vmem(104 * 8),
-        *[pltpu.SemaphoreType.DMA] * 14, *[pltpu.SemaphoreType.DMA((2 * (LAYERS - 1),))] * 2,
+        *[pltpu.SemaphoreType.DMA] * 16, *[pltpu.SemaphoreType.DMA((LAYERS - 1,))] * 2,
     ]
     inside = pl.BlockSpec(memory_space=pltpu.VMEM)
     outside = pl.BlockSpec(memory_space=pl.ANY)

time: 28.7 us -> 28.2 us (0.983)
  Pallas kernels: 27.6 us -> 27.1 us
    pallas_call x1, Pallas kernels: 27.6 us -> 27.1 us  [body(): pl.pallas_call(kernel, out_shape=pltpu.VMEM(fields, f32), in_specs=[outsi...]
where the time goes in v5:
time: 28.2 us; the launch traced here: 27.8 us
  Pallas kernels  27.1 us (96%)
  local copies, waits for them, and re-layouts  0.64 us (2%)
    pallas_call x1, Pallas kernels, body(): pl.pallas_call(kernel, out_shape=pltpu.VMEM(fields, f32), in_specs=[outsi...  27.1 us
    unnamed x1, local copies, waits for them, and re-layouts  0.64 us

profile of v5, /device:TPU:2, one launch (start us, length us, event | category | flops | bytes accessed | tf_op | source)
XLA Modules:
  0.0 27.8 jit_solution(9564886461109749902)
XLA Ops:
  0.0 27.1 %shard_map.82 = f32[5,32,128]{2,1,0:T(8,128)S(1)} custom-call(f32[5,32,128]{2,1,0:T(8,128)} %bitcast.11, f32[5,5,32,128]{3,2,1,0:T(8,128)} %bitcast.9, f32[5,32,128]{2,1,0:T(8,128)} %bitcast.12, f32[5,6,5]{2,1,0:T(8,128)} %bitcast.13, f32[50,2,512]{2,1,0:T(2,128)} %bitcast.10, s32[2]{0:T(128)} %cutoffs_in.1, bf16[1024,128]{1,0:T(8,128)(2,1)} %constant.4.clone.const_in, ...), custom_call_target="tpu_custom_call" | custom-call | tf_op jit(solution)/shard_map/pallas_call | solution.py:509
  27.1 0.6 %copy.10 = f32[5,4,8,128]{3,2,1,0:T(8,128)} copy(f32[5,4,8,128]{3,2,1,0:T(8,128)S(1)} %bitcast.8) | data formatting | bytes 163840

commit v6 on v5

--- a/solution.py
+++ b/solution.py
@@ -119,7 +119,7 @@
     residual_in, inverse_in, prior_in, coupling_in, characteristic_in, cutoffs_in, const_in, turns_in, out,
     residual, inverse, prior, coupling, cutoffs, characteristic, const, turns, load_s,
     lower, upper, edge_low, edge_high, planes_out, planes_in, ordered, corr_out, corr_in,
-    maps_out, maps_in, packed, layer_maps, vecs_out, vecs_in, layer_vecs, entry_out, entry_in,
+    maps_out, maps_in, packed, layer_maps, vecs_early, vecs_out, vecs_in, layer_vecs, entry_out, entry_in,
     down, up, first, second, third, next_reach, next_both, source, base, flat, spectra,
     pitch_s, pitch_r, back_s, back_r, side_s, side_r,
     gm_s, gm_r, zm_s, zm_r, gv_s, gv_r, zv_s, zv_r, ge_s, ge_r, zt_s, zt_r,
@@ -129,6 +129,9 @@
     layer = span // GROUP
     member = span % GROUP
 
+    def cell(m):
+        return (1 - m // 2) * (1 - m) + m // 2 * m
+
     def at_pitch(d):
         return {"pitch": lax.rem(pitch + d, PITCH), "span": span}
 
@@ -141,20 +144,18 @@
     peers = [at_pitch(d) for d in range(1, PITCH)]
     peers += [at_member(d) for d in range(1, GROUP)]
     peers += [at_layer(d) for d in range(1, LAYERS)]
-    packed[...] = jnp.zeros_like(packed)
-    for area in (planes_in, maps_in, layer_maps, vecs_in, layer_vecs, entry_in):
-        area[...] = jnp.zeros_like(area)
+    loads = [pltpu.make_async_copy(residual_in, residual, load_s.at[0])]
+    loads[0].start()
     barrier = pltpu.get_barrier_semaphore()
     for peer in peers:
         pl.semaphore_signal(barrier, inc=1, device_id=peer, device_id_type=pl.DeviceIdType.MESH)
 
-    loads = []
     for n, (src, dst) in enumerate((
-        (residual_in, residual), (prior_in, prior), (inverse_in, inverse),
+        (prior_in, prior), (inverse_in, inverse),
         (characteristic_in, characteristic), (const_in, const), (turns_in, turns),
         (coupling_in, coupling), (cutoffs_in, cutoffs),
     )):
-        loads.append(pltpu.make_async_copy(src, dst, load_s.at[n]))
+        loads.append(pltpu.make_async_copy(src, dst, load_s.at[n + 1]))
         loads[-1].start()
 
     def send(src, dst, send_sem, recv_sem, peer):
@@ -164,37 +165,20 @@
         )
         copy.start()
 
+    def to_layer(src, dst, send_sem, recv_sem, t):
+        return pltpu.make_async_remote_copy(
+            src_ref=src, dst_ref=dst, send_sem=send_sem, recv_sem=recv_sem,
+            device_id={"pitch": pitch, "span": t * GROUP + member}, device_id_type=pl.DeviceIdType.MESH,
+        )
+
     def finish(sem, count):
         area = maps_out.at[pl.ds(0, count)]
         pltpu.make_async_copy(area, area, sem).wait()
 
-    planes_out[...] = jnp.zeros_like(planes_out)
-    maps_out[...] = jnp.zeros_like(maps_out)
-    vecs_out[...] = jnp.zeros_like(vecs_out)
     loads[0].wait()
     for q, axial in enumerate((0, GROUP - 1)):
         for j in range(V):
             planes_out[every(q * V + j, LINE), :] = residual[j, axial * 8 : axial * 8 + 8, :]
-
-    pl.semaphore_wait(barrier, len(peers))
-
-    for d in FAR_FIRST:
-        to = lax.rem(pitch + d, PITCH)
-        send(
-            planes_out.at[rows(to * LINE, SENT)], planes_in.at[rows(pitch * LINE, SENT)],
-            pitch_s, pitch_r, at_pitch(d),
-        )
-    loads[1].wait()
-    column = lax.broadcasted_iota(jnp.int32, (8, LANES), 1)
-    last = initial = jnp.zeros((8, LANES), jnp.float32)
-    for n in range(V * GROUP):
-        tile = prior[n // GROUP, n % GROUP * 8 : n % GROUP * 8 + 8, :]
-        last = jnp.where(column == n, pltpu.roll(tile, n + 1, 1), last)
-        initial = jnp.where(column == n, pltpu.roll(tile, n, 1) if n else tile, initial)
-    edge_high[...] = last
-    edge_low[...] = initial
-    send(edge_high, lower, side_s, side_r, at_pitch(1))
-    send(edge_low, upper, side_s, side_r, at_pitch(PITCH - 1))
 
     loads[2].wait()
     loads[6].wait()
@@ -205,6 +189,16 @@
         up[s] = scaled(block, coupling, 1)
         reach = down[s] if s == 0 else product(down[s], reach)
         first[s] = reach
+
+    pl.semaphore_wait(barrier, len(peers))
+
+    for d in FAR_FIRST:
+        to = lax.rem(pitch + d, PITCH)
+        send(
+            planes_out.at[rows(to * LINE, SENT)], planes_in.at[rows(pitch * LINE, SENT)],
+            pitch_s, pitch_r, at_pitch(d),
+        )
+    reach = first[3]
     both = reach
     trail = up[3]
     second[3] = both
@@ -226,15 +220,26 @@
             maps_out[every(A + V * k + i, MAPS), :] = reach[k, i]
             maps_out[every(B + V * k + i, MAPS), :] = trail[k, i]
             maps_out[every(C + V * k + i, MAPS), :] = both[k, i]
-
     for d in MEMBERS:
         to = lax.rem(member + d, GROUP)
         send(
-            maps_out.at[rows(to * 2 * MAPS, USED)], maps_in.at[rows(member * MAPS, USED)],
+            maps_out.at[rows(cell(to) * 2 * MAPS, USED)], maps_in.at[rows(member * MAPS, USED)],
             gm_s, gm_r, at_member(d),
         )
+    loads[1].wait()
+    column = lax.broadcasted_iota(jnp.int32, (8, LANES), 1)
+    last = initial = jnp.zeros((8, LANES), jnp.float32)
+    for n in range(V * GROUP):
+        tile = prior[n // GROUP, n % GROUP * 8 : n % GROUP * 8 + 8, :]
+        last = jnp.where(column == n, pltpu.roll(tile, n + 1, 1), last)
+        initial = jnp.where(column == n, pltpu.roll(tile, n, 1) if n else tile, initial)
+    edge_high[...] = last
+    edge_low[...] = initial
+    send(edge_high, lower, side_s, side_r, at_pitch(1))
+    send(edge_low, upper, side_s, side_r, at_pitch(PITCH - 1))
+
     planes_in[rows(pitch * LINE, LINE), :] = planes_out[rows(pitch * LINE, LINE), :]
-    maps_in[rows(member * MAPS, MAPS), :] = maps_out[rows(member * 2 * MAPS, MAPS), :]
+    maps_in[rows(member * MAPS, MAPS), :] = maps_out[rows(cell(member) * 2 * MAPS, MAPS), :]
 
     loads[3].wait()
     flat[100:104, :] = jnp.zeros((4, 512), jnp.float32)
@@ -332,18 +337,16 @@
         packed[start : start + 8, :] = columns[n]
     layer_maps[rows(layer * MAPS, MAPS), :] = packed[...]
     lower_copies = []
-    for d in FAR_FIRST:
-        send(
-            layer_maps.at[rows(layer * MAPS + A, SINGLE)], layer_maps.at[rows(layer * MAPS + A, SINGLE)],
-            zm_s, zm_r, at_layer(d),
-        )
-        copy = pltpu.make_async_remote_copy(
-            src_ref=layer_maps.at[rows(layer * MAPS, PAIR)], dst_ref=layer_maps.at[rows(layer * MAPS, PAIR)],
-            send_sem=zt_s.at[d - 1], recv_sem=zt_r.at[d - 1],
-            device_id=at_layer(d), device_id_type=pl.DeviceIdType.MESH,
-        )
-        lower_copies.append((copy, layer + d >= LAYERS, layer < d))
-        pl.when(layer + d >= LAYERS)(copy.start)
+    for t in range(LAYERS):
+        single = to_layer(
+            layer_maps.at[rows(layer * MAPS + A, SINGLE)], layer_maps.at[rows(layer * MAPS + A, SINGLE)], zm_s, zm_r, t,
+        )
+        pl.when(layer != t)(single.start)
+        pair = to_layer(
+            layer_maps.at[rows(layer * MAPS, PAIR)], layer_maps.at[rows(layer * MAPS, PAIR)], zt_s.at[t], zt_r.at[layer], t,
+        )
+        pl.when(layer > t)(pair.start)
+        lower_copies.append(pair)
 
     finish(side_r, 16)
     own = prior[...]
@@ -372,35 +375,42 @@
         total = total - jnp.concatenate([zero_row, before[:24]], 0) - jnp.concatenate([after[8:], zero_row], 0)
         source[i] = total
 
+    def sweep(offsets, parity):
+        star = None
+        for s in range(4):
+            block = inverse[:, :, every(s, 4), :]
+            rhs = source[:, every(s, 4), :]
+            value = block[:, 0] * rhs[0][None]
+            for j in range(1, V):
+                value = value + block[:, j] * rhs[j][None]
+            star = value if s == 0 else value + apply(down[s], star)
+            base[s] = star
+        update = star
+        for s in (2, 1, 0):
+            update = base[s] + apply(up[s], update)
+            base[s] = update
+        ahead = pltpu.roll(star, 7, 1) + apply(next_reach, star)
+        behind = update + apply(third[0], pltpu.roll(update, 7, 1) + apply(next_both, star))
+        for i in range(V):
+            offsets[every(i, VECS), :] = ahead[i]
+            offsets[every(V + i, VECS), :] = behind[i]
+        for d in MEMBERS:
+            to = lax.rem(member + d, GROUP)
+            copy = pltpu.make_async_remote_copy(
+                src_ref=offsets.at[rows(cell(to) * 2 * VECS, SENT)], dst_ref=vecs_in.at[rows(member * VECS, SENT)],
+                send_sem=gv_s, recv_sem=gv_r,
+                device_id=at_member(d), device_id_type=pl.DeviceIdType.MESH,
+            )
+            pl.when(lax.rem(to, 2) == parity)(copy.start)
+
+    sweep(vecs_early, 0)
+
     finish(back_r, (PITCH - 1) * SENT)
     for j in range(V):
         source[j, 0:8, :] = source[j, 0:8, :] + corr_in[every(j, LINE), :]
         source[j, 24:32, :] = source[j, 24:32, :] + corr_in[every(V + j, LINE), :]
-    star = None
-    for s in range(4):
-        block = inverse[:, :, every(s, 4), :]
-        rhs = source[:, every(s, 4), :]
-        value = block[:, 0] * rhs[0][None]
-        for j in range(1, V):
-            value = value + block[:, j] * rhs[j][None]
-        star = value if s == 0 else value + apply(down[s], star)
-        base[s] = star
-    update = star
-    for s in (2, 1, 0):
-        update = base[s] + apply(up[s], update)
-        base[s] = update
-    ahead = pltpu.roll(star, 7, 1) + apply(next_reach, star)
-    behind = update + apply(third[0], pltpu.roll(update, 7, 1) + apply(next_both, star))
-    for i in range(V):
-        vecs_out[every(i, VECS), :] = ahead[i]
-        vecs_out[every(V + i, VECS), :] = behind[i]
-    for d in MEMBERS:
-        to = lax.rem(member + d, GROUP)
-        send(
-            vecs_out.at[rows(to * 2 * VECS, SENT)], vecs_in.at[rows(member * VECS, SENT)],
-            gv_s, gv_r, at_member(d),
-        )
-    vecs_in[rows(member * VECS, VECS), :] = vecs_out[rows(member * 2 * VECS, VECS), :]
+    sweep(vecs_out, 1)
+    vecs_in[rows(member * VECS, VECS), :] = vecs_out[rows(cell(member) * 2 * VECS, VECS), :]
 
     def chain(count, maps_ref, vecs_ref, x, y):
         entering_x, entering_y, crossing = [], [None] * count, []
@@ -425,14 +435,14 @@
     tail = pltpu.roll(y, V, 0)
     layer_vecs[rows(layer * VECS, 8), :] = jnp.where(place < V, x, tail)
     layer_vecs[rows(layer * VECS + 8, 8), :] = tail
-    for d in FAR_FIRST:
-        send(
-            layer_vecs.at[rows(layer * VECS, SENT)], layer_vecs.at[rows(layer * VECS, SENT)],
-            zv_s, zv_r, at_layer(d),
-        )
+    for t in range(LAYERS):
+        pl.when(layer != t)(to_layer(
+            layer_vecs.at[rows(layer * VECS, SENT)], layer_vecs.at[rows(layer * VECS, SENT)], zv_s, zv_r, t,
+        ).start)
     finish(zm_r, (LAYERS - 1) * SINGLE)
-    for copy, _, from_above in lower_copies:
-        pl.when(from_above)(copy.wait_recv)
+    for t in range(LAYERS):
+        above = layer_maps.at[pl.ds(t * MAPS, PAIR)]
+        pl.when(layer < t)(to_layer(above, above, zt_s.at[t], zt_r.at[t], t).wait_recv)
     finish(zv_r, (LAYERS - 1) * SENT)
     entering_x, entering_y, _, _ = chain(LAYERS, layer_maps, layer_vecs, None, None)
     x = jnp.zeros((8, LANES), jnp.float32)
@@ -450,10 +460,10 @@
     for d in MEMBERS:
         to = lax.rem(member + d, GROUP)
         send(
-            entry_out.at[rows(to * VECS, SENT)], entry_in.at[rows(member * 2 * VECS, SENT)],
+            entry_out.at[rows(to * VECS, SENT)], entry_in.at[rows(cell(member) * 2 * VECS, SENT)],
             ge_s, ge_r, at_member(d),
         )
-    entry_in[rows(member * 2 * VECS, VECS), :] = entry_out[rows(member * VECS, VECS), :]
+    entry_in[rows(cell(member) * 2 * VECS, VECS), :] = entry_out[rows(member * VECS, VECS), :]
     finish(ge_r, (GROUP - 1) * SENT)
     x = jnp.stack([entry_in[every(i, VECS), :] for i in range(V)])
     y = jnp.stack([entry_in[every(V + i, VECS), :] for i in range(V)])
@@ -476,8 +486,8 @@
     finish(zv_s, (LAYERS - 1) * SENT)
     finish(ge_s, (GROUP - 1) * SENT)
     finish(zm_s, (LAYERS - 1) * SINGLE)
-    for copy, wraps, _ in lower_copies:
-        pl.when(wraps)(copy.wait_send)
+    for t, pair in enumerate(lower_copies):
+        pl.when(layer > t)(pair.wait_send)
 
 
 def body(residual, inverse_diagonal, prior_increment, coupling, characteristic, cutoffs):
@@ -496,12 +506,12 @@
         vmem(8), vmem(8), vmem(8), vmem(8),
         vmem(128), vmem(128), vmem(128), vmem(128), vmem(128),
         vmem(8 * MAPS), vmem(GROUP * MAPS), vmem(MAPS), vmem(LAYERS * MAPS),
-        vmem(8 * VECS), vmem(GROUP * VECS), vmem(LAYERS * VECS), vmem(GROUP * VECS), vmem(8 * VECS),
+        vmem(8 * VECS), vmem(8 * VECS), vmem(GROUP * VECS), vmem(LAYERS * VECS), vmem(GROUP * VECS), vmem(8 * VECS),
         matrices, matrices, matrices, matrices, matrices,
         pltpu.VMEM((V, V, 8, LANES), f32), pltpu.VMEM((V, V, 8, LANES), f32),
         pltpu.VMEM(fields, f32), pltpu.VMEM((4, V, 8, LANES), f32),
         pltpu.VMEM((104, 512), f32), vmem(104 * 8),
-        *[pltpu.SemaphoreType.DMA] * 16, *[pltpu.SemaphoreType.DMA((LAYERS - 1,))] * 2,
+        *[pltpu.SemaphoreType.DMA] * 16, *[pltpu.SemaphoreType.DMA((LAYERS,))] * 2,
     ]
     inside = pl.BlockSpec(memory_space=pltpu.VMEM)
     outside = pl.BlockSpec(memory_space=pl.ANY)

time: 28.2 us -> 27.6 us (0.979)
  Pallas kernels: 27.1 us -> 26.7 us
    pallas_call x1, Pallas kernels: 27.1 us -> 26.7 us  [body(): pl.pallas_call(kernel, out_shape=pltpu.VMEM(fields, f32), in_specs=[outsi...]
where the time goes in v6:
time: 27.6 us; the launch traced here: 27.4 us
  Pallas kernels  26.7 us (97%)
  local copies, waits for them, and re-layouts  0.64 us (2%)
    pallas_call x1, Pallas kernels, body(): pl.pallas_call(kernel, out_shape=pltpu.VMEM(fields, f32), in_specs=[outsi...  26.7 us
    unnamed x1, local copies, waits for them, and re-layouts  0.64 us

profile of v6, /device:TPU:2, one launch (start us, length us, event | category | flops | bytes accessed | tf_op | source)
XLA Modules:
  0.0 27.4 jit_solution(9701146007196265005)
XLA Ops:
  0.0 26.7 %shard_map.82 = f32[5,32,128]{2,1,0:T(8,128)S(1)} custom-call(f32[5,32,128]{2,1,0:T(8,128)} %bitcast.11, f32[5,5,32,128]{3,2,1,0:T(8,128)} %bitcast.9, f32[5,32,128]{2,1,0:T(8,128)} %bitcast.12, f32[5,6,5]{2,1,0:T(8,128)} %bitcast.13, f32[50,2,512]{2,1,0:T(2,128)} %bitcast.10, s32[2]{0:T(128)} %cutoffs_in.1, bf16[1024,128]{1,0:T(8,128)(2,1)} %constant.4.clone.const_in, ...), custom_call_target="tpu_custom_call" | custom-call | tf_op jit(solution)/shard_map/pallas_call | solution.py:519
  26.7 0.6 %copy.10 = f32[5,4,8,128]{3,2,1,0:T(8,128)} copy(f32[5,4,8,128]{3,2,1,0:T(8,128)S(1)} %bitcast.8) | data formatting | bytes 163840

commit v7 on v6

--- a/solution.py
+++ b/solution.py
@@ -1,3 +1,5 @@
+import functools
+
 import jax
 import jax.numpy as jnp
 import numpy as np
@@ -336,17 +338,15 @@
         start = A + V * n if n < V else V * n - 25
         packed[start : start + 8, :] = columns[n]
     layer_maps[rows(layer * MAPS, MAPS), :] = packed[...]
-    lower_copies = []
     for t in range(LAYERS):
         single = to_layer(
             layer_maps.at[rows(layer * MAPS + A, SINGLE)], layer_maps.at[rows(layer * MAPS + A, SINGLE)], zm_s, zm_r, t,
         )
         pl.when(layer != t)(single.start)
         pair = to_layer(
-            layer_maps.at[rows(layer * MAPS, PAIR)], layer_maps.at[rows(layer * MAPS, PAIR)], zt_s.at[t], zt_r.at[layer], t,
+            layer_maps.at[rows(layer * MAPS, PAIR)], layer_maps.at[rows(layer * MAPS, PAIR)], zt_s, zt_r, t,
         )
         pl.when(layer > t)(pair.start)
-        lower_copies.append(pair)
 
     finish(side_r, 16)
     own = prior[...]
@@ -440,9 +440,8 @@
             layer_vecs.at[rows(layer * VECS, SENT)], layer_vecs.at[rows(layer * VECS, SENT)], zv_s, zv_r, t,
         ).start)
     finish(zm_r, (LAYERS - 1) * SINGLE)
-    for t in range(LAYERS):
-        above = layer_maps.at[pl.ds(t * MAPS, PAIR)]
-        pl.when(layer < t)(to_layer(above, above, zt_s.at[t], zt_r.at[t], t).wait_recv)
+    for t in range(LAYERS - 1):
+        pl.when(layer == t)(functools.partial(finish, zt_r, (LAYERS - 1 - t) * PAIR))
     finish(zv_r, (LAYERS - 1) * SENT)
     entering_x, entering_y, _, _ = chain(LAYERS, layer_maps, layer_vecs, None, None)
     x = jnp.zeros((8, LANES), jnp.float32)
@@ -486,8 +485,8 @@
     finish(zv_s, (LAYERS - 1) * SENT)
     finish(ge_s, (GROUP - 1) * SENT)
     finish(zm_s, (LAYERS - 1) * SINGLE)
-    for t, pair in enumerate(lower_copies):
-        pl.when(layer > t)(pair.wait_send)
+    for t in range(1, LAYERS):
+        pl.when(layer == t)(functools.partial(finish, zt_s, t * PAIR))
 
 
 def body(residual, inverse_diagonal, prior_increment, coupling, characteristic, cutoffs):
@@ -511,7 +510,7 @@
         pltpu.VMEM((V, V, 8, LANES), f32), pltpu.VMEM((V, V, 8, LANES), f32),
         pltpu.VMEM(fields, f32), pltpu.VMEM((4, V, 8, LANES), f32),
         pltpu.VMEM((104, 512), f32), vmem(104 * 8),
-        *[pltpu.SemaphoreType.DMA] * 16, *[pltpu.SemaphoreType.DMA((LAYERS,))] * 2,
+        *[pltpu.SemaphoreType.DMA] * 18,
     ]
     inside = pl.BlockSpec(memory_space=pltpu.VMEM)
     outside = pl.BlockSpec(memory_space=pl.ANY)

time: 27.6 us -> 27.4 us (level)
  no operation moved by 1% of the time
where the time goes in v7:
time: 27.4 us; the launch traced here: 27.2 us
  Pallas kernels  26.6 us (97%)
  local copies, waits for them, and re-layouts  0.64 us (2%)
    pallas_call x1, Pallas kernels, body(): pl.pallas_call(kernel, out_shape=pltpu.VMEM(fields, f32), in_specs=[outsi...  26.6 us
    unnamed x1, local copies, waits for them, and re-layouts  0.64 us

profile of v7, /device:TPU:2, one launch (start us, length us, event | category | flops | bytes accessed | tf_op | source)
XLA Modules:
  0.0 27.2 jit_solution(17066253814210575203)
XLA Ops:
  0.0 26.6 %shard_map.82 = f32[5,32,128]{2,1,0:T(8,128)S(1)} custom-call(f32[5,32,128]{2,1,0:T(8,128)} %bitcast.11, f32[5,5,32,128]{3,2,1,0:T(8,128)} %bitcast.9, f32[5,32,128]{2,1,0:T(8,128)} %bitcast.12, f32[5,6,5]{2,1,0:T(8,128)} %bitcast.13, f32[50,2,512]{2,1,0:T(2,128)} %bitcast.10, s32[2]{0:T(128)} %cutoffs_in.1, bf16[1024,128]{1,0:T(8,128)(2,1)} %constant.4.clone.const_in, ...), custom_call_target="tpu_custom_call" | custom-call | tf_op jit(solution)/shard_map/pallas_call | solution.py:518
  26.6 0.6 %copy.10 = f32[5,4,8,128]{3,2,1,0:T(8,128)} copy(f32[5,4,8,128]{3,2,1,0:T(8,128)S(1)} %bitcast.8) | data formatting | bytes 163840

commit v8 on v7

--- a/solution.py
+++ b/solution.py
@@ -124,7 +124,7 @@
     maps_out, maps_in, packed, layer_maps, vecs_early, vecs_out, vecs_in, layer_vecs, entry_out, entry_in,
     down, up, first, second, third, next_reach, next_both, source, base, flat, spectra,
     pitch_s, pitch_r, back_s, back_r, side_s, side_r,
-    gm_s, gm_r, zm_s, zm_r, gv_s, gv_r, zv_s, zv_r, ge_s, ge_r, zt_s, zt_r,
+    gm_s, gm_r, zm_s, zm_r, gv_s, gv_r, zv_s, zv_r, ge_s, ge_r, zt_s, zt_r, ready,
 ):
     pitch = lax.axis_index("pitch")
     span = lax.axis_index("span")
@@ -145,7 +145,8 @@
 
     peers = [at_pitch(d) for d in range(1, PITCH)]
     peers += [at_member(d) for d in range(1, GROUP)]
-    peers += [at_layer(d) for d in range(1, LAYERS)]
+    near = [at_layer(d) for d in (1, 2, LAYERS - 2, LAYERS - 1)]
+    peers += near
     loads = [pltpu.make_async_copy(residual_in, residual, load_s.at[0])]
     loads[0].start()
     barrier = pltpu.get_barrier_semaphore()
@@ -228,6 +229,8 @@
             maps_out.at[rows(cell(to) * 2 * MAPS, USED)], maps_in.at[rows(member * MAPS, USED)],
             gm_s, gm_r, at_member(d),
         )
+    for peer in near:
+        pl.semaphore_signal(ready, inc=1, device_id=peer, device_id_type=pl.DeviceIdType.MESH)
     loads[1].wait()
     column = lax.broadcasted_iota(jnp.int32, (8, LANES), 1)
     last = initial = jnp.zeros((8, LANES), jnp.float32)
@@ -338,6 +341,7 @@
         start = A + V * n if n < V else V * n - 25
         packed[start : start + 8, :] = columns[n]
     layer_maps[rows(layer * MAPS, MAPS), :] = packed[...]
+    pl.semaphore_wait(ready, len(near))
     for t in range(LAYERS):
         single = to_layer(
             layer_maps.at[rows(layer * MAPS + A, SINGLE)], layer_maps.at[rows(layer * MAPS + A, SINGLE)], zm_s, zm_r, t,
@@ -511,6 +515,7 @@
         pltpu.VMEM(fields, f32), pltpu.VMEM((4, V, 8, LANES), f32),
         pltpu.VMEM((104, 512), f32), vmem(104 * 8),
         *[pltpu.SemaphoreType.DMA] * 18,
+        pltpu.SemaphoreType.REGULAR,
     ]
     inside = pl.BlockSpec(memory_space=pltpu.VMEM)
     outside = pl.BlockSpec(memory_space=pl.ANY)

time: 27.4 us -> 27.4 us (level)
  no operation moved by 1% of the time
where the time goes in v8:
time: 27.4 us; the launch traced here: 27.2 us
  Pallas kernels  26.6 us (97%)
  local copies, waits for them, and re-layouts  0.64 us (2%)
    pallas_call x1, Pallas kernels, body(): pl.pallas_call(kernel, out_shape=pltpu.VMEM(fields, f32), in_specs=[outsi...  26.6 us
    unnamed x1, local copies, waits for them, and re-layouts  0.64 us

profile of v8, /device:TPU:2, one launch (start us, length us, event | category | flops | bytes accessed | tf_op | source)
XLA Modules:
  0.0 27.2 jit_solution(14858873225380129781)
XLA Ops:
  0.0 26.6 %shard_map.82 = f32[5,32,128]{2,1,0:T(8,128)S(1)} custom-call(f32[5,32,128]{2,1,0:T(8,128)} %bitcast.11, f32[5,5,32,128]{3,2,1,0:T(8,128)} %bitcast.9, f32[5,32,128]{2,1,0:T(8,128)} %bitcast.12, f32[5,6,5]{2,1,0:T(8,128)} %bitcast.13, f32[50,2,512]{2,1,0:T(2,128)} %bitcast.10, s32[2]{0:T(128)} %cutoffs_in.1, bf16[1024,128]{1,0:T(8,128)(2,1)} %constant.4.clone.const_in, ...), custom_call_target="tpu_custom_call" | custom-call | tf_op jit(solution)/shard_map/pallas_call | solution.py:523
  26.6 0.6 %copy.10 = f32[5,4,8,128]{3,2,1,0:T(8,128)} copy(f32[5,4,8,128]{3,2,1,0:T(8,128)S(1)} %bitcast.8) | data formatting | bytes 163840

commit v9 on v8

--- a/solution.py
+++ b/solution.py
@@ -21,7 +21,7 @@
 SENT = 10
 LANES = 128
 
-FORWARD, BACK_RE, BACK_IM, LOW = 0, 256, 384, 512
+FORWARD, BACK_RE, BACK_IM, ROWS = 0, 768, 1152, 1536
 HALF = float(np.sqrt(0.5))
 
 
@@ -37,11 +37,13 @@
     back_re = np.concatenate([cos.T, -sin.T], 0)
     back_im = np.concatenate([sin.T, cos.T], 0)
     parts = [forward, back_re, back_im]
-    whole = np.concatenate(parts, 0).astype(np.float32)
-    high = whole.astype(jnp.bfloat16)
-    low = (whole - high.astype(np.float32)).astype(jnp.bfloat16)
+    pieces = []
+    for part in parts:
+        whole = part.astype(np.float32)
+        high = whole.astype(jnp.bfloat16)
+        pieces += [high, high, (whole - high.astype(np.float32)).astype(jnp.bfloat16)]
     turns = np.concatenate([np.cos(twiddle), np.sin(twiddle)], 0).astype(np.float32)
-    return np.concatenate([high, low], 0), turns
+    return np.concatenate(pieces, 0), turns
 
 
 FAR_FIRST = (4, 3, 5, 2, 6, 1, 7)
@@ -83,11 +85,8 @@
 def times(data, const, start, size):
     data_high = data.astype(jnp.bfloat16)
     data_low = (data - data_high.astype(jnp.float32)).astype(jnp.bfloat16)
-    high = const[start : start + size, :]
-    low = const[LOW + start : LOW + start + size, :]
-    total = jnp.dot(data_high, high, preferred_element_type=jnp.float32)
-    total = total + jnp.dot(data_low, high, preferred_element_type=jnp.float32)
-    return total + jnp.dot(data_high, low, preferred_element_type=jnp.float32)
+    thrice = jnp.concatenate([data_high, data_low, data_high], 1)
+    return jnp.dot(thrice, const[start : start + 3 * size, :], preferred_element_type=jnp.float32)
 
 
 def eight_forward(x):
@@ -123,8 +122,8 @@
     lower, upper, edge_low, edge_high, planes_out, planes_in, ordered, corr_out, corr_in,
     maps_out, maps_in, packed, layer_maps, vecs_early, vecs_out, vecs_in, layer_vecs, entry_out, entry_in,
     down, up, first, second, third, next_reach, next_both, source, base, flat, spectra,
-    pitch_s, pitch_r, back_s, back_r, side_s, side_r,
-    gm_s, gm_r, zm_s, zm_r, gv_s, gv_r, zv_s, zv_r, ge_s, ge_r, zt_s, zt_r, ready,
+    sent, pitch_r, back_r, side_r,
+    gm_r, zm_r, gv_r, zv_r, ge_r, zt_s, zt_r, ready,
 ):
     pitch = lax.axis_index("pitch")
     span = lax.axis_index("span")
@@ -199,7 +198,7 @@
         to = lax.rem(pitch + d, PITCH)
         send(
             planes_out.at[rows(to * LINE, SENT)], planes_in.at[rows(pitch * LINE, SENT)],
-            pitch_s, pitch_r, at_pitch(d),
+            sent, pitch_r, at_pitch(d),
         )
     reach = first[3]
     both = reach
@@ -227,7 +226,7 @@
         to = lax.rem(member + d, GROUP)
         send(
             maps_out.at[rows(cell(to) * 2 * MAPS, USED)], maps_in.at[rows(member * MAPS, USED)],
-            gm_s, gm_r, at_member(d),
+            sent, gm_r, at_member(d),
         )
     for peer in near:
         pl.semaphore_signal(ready, inc=1, device_id=peer, device_id_type=pl.DeviceIdType.MESH)
@@ -240,8 +239,8 @@
         initial = jnp.where(column == n, pltpu.roll(tile, n, 1) if n else tile, initial)
     edge_high[...] = last
     edge_low[...] = initial
-    send(edge_high, lower, side_s, side_r, at_pitch(1))
-    send(edge_low, upper, side_s, side_r, at_pitch(PITCH - 1))
+    send(edge_high, lower, sent, side_r, at_pitch(1))
+    send(edge_low, upper, sent, side_r, at_pitch(PITCH - 1))
 
     planes_in[rows(pitch * LINE, LINE), :] = planes_out[rows(pitch * LINE, LINE), :]
     maps_in[rows(member * MAPS, MAPS), :] = maps_out[rows(cell(member) * 2 * MAPS, MAPS), :]
@@ -306,7 +305,7 @@
         to = lax.rem(pitch + d, PITCH)
         send(
             corr_out.at[rows(to * LINE, SENT)], corr_in.at[rows(pitch * LINE, SENT)],
-            back_s, back_r, at_pitch(d),
+            sent, back_r, at_pitch(d),
         )
     corr_in[rows(pitch * LINE, LINE), :] = corr_out[rows(pitch * LINE, LINE), :]
 
@@ -344,7 +343,7 @@
     pl.semaphore_wait(ready, len(near))
     for t in range(LAYERS):
         single = to_layer(
-            layer_maps.at[rows(layer * MAPS + A, SINGLE)], layer_maps.at[rows(layer * MAPS + A, SINGLE)], zm_s, zm_r, t,
+            layer_maps.at[rows(layer * MAPS + A, SINGLE)], layer_maps.at[rows(layer * MAPS + A, SINGLE)], sent, zm_r, t,
         )
         pl.when(layer != t)(single.start)
         pair = to_layer(
@@ -402,7 +401,7 @@
             to = lax.rem(member + d, GROUP)
             copy = pltpu.make_async_remote_copy(
                 src_ref=offsets.at[rows(cell(to) * 2 * VECS, SENT)], dst_ref=vecs_in.at[rows(member * VECS, SENT)],
-                send_sem=gv_s, recv_sem=gv_r,
+                send_sem=sent, recv_sem=gv_r,
                 device_id=at_member(d), device_id_type=pl.DeviceIdType.MESH,
             )
             pl.when(lax.rem(to, 2) == parity)(copy.start)
@@ -441,7 +440,7 @@
     layer_vecs[rows(layer * VECS + 8, 8), :] = tail
     for t in range(LAYERS):
         pl.when(layer != t)(to_layer(
-            layer_vecs.at[rows(layer * VECS, SENT)], layer_vecs.at[rows(layer * VECS, SENT)], zv_s, zv_r, t,
+            layer_vecs.at[rows(layer * VECS, SENT)], layer_vecs.at[rows(layer * VECS, SENT)], sent, zv_r, t,
         ).start)
     finish(zm_r, (LAYERS - 1) * SINGLE)
     for t in range(LAYERS - 1):
@@ -464,7 +463,7 @@
         to = lax.rem(member + d, GROUP)
         send(
             entry_out.at[rows(to * VECS, SENT)], entry_in.at[rows(cell(member) * 2 * VECS, SENT)],
-            ge_s, ge_r, at_member(d),
+            sent, ge_r, at_member(d),
         )
     entry_in[rows(cell(member) * 2 * VECS, VECS), :] = entry_out[rows(member * VECS, VECS), :]
     finish(ge_r, (GROUP - 1) * SENT)
@@ -481,14 +480,8 @@
         for i in range(V):
             out[i, every(s, 4), :] = value[i]
 
-    finish(pitch_s, (PITCH - 1) * SENT)
-    finish(side_s, 16)
-    finish(gm_s, (GROUP - 1) * USED)
-    finish(back_s, (PITCH - 1) * SENT)
-    finish(gv_s, (GROUP - 1) * SENT)
-    finish(zv_s, (LAYERS - 1) * SENT)
-    finish(ge_s, (GROUP - 1) * SENT)
-    finish(zm_s, (LAYERS - 1) * SINGLE)
+    total = 16 + (2 * PITCH - 2) * SENT + (GROUP - 1) * (USED + 2 * SENT) + (LAYERS - 1) * (SINGLE + SENT)
+    finish(sent, total)
     for t in range(1, LAYERS):
         pl.when(layer == t)(functools.partial(finish, zt_s, t * PAIR))
 
@@ -504,7 +497,7 @@
     scratch = [
         pltpu.VMEM(fields, f32), pltpu.VMEM((V, V, 32, LANES), f32), pltpu.VMEM(fields, f32),
         pltpu.SMEM((V, 6, V), f32), pltpu.SMEM((2,), jnp.int32),
-        pltpu.VMEM((50, 2, 512), f32), pltpu.VMEM((2 * LOW, LANES), jnp.bfloat16), vmem(16),
+        pltpu.VMEM((50, 2, 512), f32), pltpu.VMEM((ROWS, LANES), jnp.bfloat16), vmem(16),
         pltpu.SemaphoreType.DMA((8,)),
         vmem(8), vmem(8), vmem(8), vmem(8),
         vmem(128), vmem(128), vmem(128), vmem(128), vmem(128),
@@ -514,7 +507,7 @@
         pltpu.VMEM((V, V, 8, LANES), f32), pltpu.VMEM((V, V, 8, LANES), f32),
         pltpu.VMEM(fields, f32), pltpu.VMEM((4, V, 8, LANES), f32),
         pltpu.VMEM((104, 512), f32), vmem(104 * 8),
-        *[pltpu.SemaphoreType.DMA] * 18,
+        *[pltpu.SemaphoreType.DMA] * 11,
         pltpu.SemaphoreType.REGULAR,
     ]
     inside = pl.BlockSpec(memory_space=pltpu.VMEM)

time: 27.4 us -> 27.3 us (level)
  no operation moved by 1% of the time
where the time goes in v9:
time: 27.3 us; the launch traced here: 27.2 us
  Pallas kernels  26.6 us (97%)
  local copies, waits for them, and re-layouts  0.64 us (2%)
    pallas_call x1, Pallas kernels, body(): pl.pallas_call(kernel, out_shape=pltpu.VMEM(fields, f32), in_specs=[outsi...  26.6 us
    unnamed x1, local copies, waits for them, and re-layouts  0.64 us

profile of v9, /device:TPU:2, one launch (start us, length us, event | category | flops | bytes accessed | tf_op | source)
XLA Modules:
  0.0 27.2 jit_solution(7821455751150447665)
XLA Ops:
  0.0 26.6 %shard_map.82 = f32[5,32,128]{2,1,0:T(8,128)S(1)} custom-call(f32[5,32,128]{2,1,0:T(8,128)} %bitcast.11, f32[5,5,32,128]{3,2,1,0:T(8,128)} %bitcast.9, f32[5,32,128]{2,1,0:T(8,128)} %bitcast.12, f32[5,6,5]{2,1,0:T(8,128)} %bitcast.13, f32[50,2,512]{2,1,0:T(2,128)} %bitcast.10, s32[2]{0:T(128)} %cutoffs_in.1, bf16[1536,128]{1,0:T(8,128)(2,1)} %constant.4.clone.const_in, ...), custom_call_target="tpu_custom_call" | custom-call | tf_op jit(solution)/shard_map/pallas_call | solution.py:516
  26.6 0.6 %copy.10 = f32[5,4,8,128]{3,2,1,0:T(8,128)} copy(f32[5,4,8,128]{3,2,1,0:T(8,128)S(1)} %bitcast.8) | data formatting | bytes 163840

commit v10 on v8

--- a/solution.py
+++ b/solution.py
@@ -186,7 +186,7 @@
     loads[2].wait()
     loads[6].wait()
     reach = None
-    for s in range(4):
+    for s in range(2):
         block = inverse[:, :, every(s, 4), :]
         down[s] = scaled(block, coupling, 0)
         up[s] = scaled(block, coupling, 1)
@@ -201,7 +201,13 @@
             planes_out.at[rows(to * LINE, SENT)], planes_in.at[rows(pitch * LINE, SENT)],
             pitch_s, pitch_r, at_pitch(d),
         )
-    reach = first[3]
+    reach = first[1]
+    for s in (2, 3):
+        block = inverse[:, :, every(s, 4), :]
+        down[s] = scaled(block, coupling, 0)
+        up[s] = scaled(block, coupling, 1)
+        reach = product(down[s], reach)
+        first[s] = reach
     both = reach
     trail = up[3]
     second[3] = both

time: 27.4 us -> 27.5 us (level)
  no operation moved by 1% of the time
where the time goes in v10:
time: 27.5 us; the launch traced here: 27.2 us
  Pallas kernels  26.6 us (97%)
  local copies, waits for them, and re-layouts  0.64 us (2%)
    pallas_call x1, Pallas kernels, body(): pl.pallas_call(kernel, out_shape=pltpu.VMEM(fields, f32), in_specs=[outsi...  26.6 us
    unnamed x1, local copies, waits for them, and re-layouts  0.64 us

profile of v10, /device:TPU:2, one launch (start us, length us, event | category | flops | bytes accessed | tf_op | source)
XLA Modules:
  0.0 27.2 jit_solution(299859288315316167)
XLA Ops:
  0.0 26.6 %shard_map.82 = f32[5,32,128]{2,1,0:T(8,128)S(1)} custom-call(f32[5,32,128]{2,1,0:T(8,128)} %bitcast.11, f32[5,5,32,128]{3,2,1,0:T(8,128)} %bitcast.9, f32[5,32,128]{2,1,0:T(8,128)} %bitcast.12, f32[5,6,5]{2,1,0:T(8,128)} %bitcast.13, f32[50,2,512]{2,1,0:T(2,128)} %bitcast.10, s32[2]{0:T(128)} %cutoffs_in.1, bf16[1024,128]{1,0:T(8,128)(2,1)} %constant.4.clone.const_in, ...), custom_call_target="tpu_custom_call" | custom-call | tf_op jit(solution)/shard_map/pallas_call | solution.py:529
  26.6 0.6 %copy.10 = f32[5,4,8,128]{3,2,1,0:T(8,128)} copy(f32[5,4,8,128]{3,2,1,0:T(8,128)S(1)} %bitcast.8) | data formatting | bytes 163840

commit v11 on v8

--- a/solution.py
+++ b/solution.py
@@ -45,7 +45,7 @@
 
 
 FAR_FIRST = (4, 3, 5, 2, 6, 1, 7)
-MEMBERS = (2, 1, 3)
+MEMBERS = (1, 3, 2)
 
 
 def every(start, stride):

time: 27.4 us -> 27.4 us (level)
  no operation moved by 1% of the time
where the time goes in v11:
time: 27.4 us; the launch traced here: 27.3 us
  Pallas kernels  26.6 us (97%)
  local copies, waits for them, and re-layouts  0.64 us (2%)
    pallas_call x1, Pallas kernels, body(): pl.pallas_call(kernel, out_shape=pltpu.VMEM(fields, f32), in_specs=[outsi...  26.6 us
    unnamed x1, local copies, waits for them, and re-layouts  0.64 us

profile of v11, /device:TPU:2, one launch (start us, length us, event | category | flops | bytes accessed | tf_op | source)
XLA Modules:
  0.0 27.3 jit_solution(4583031059698330740)
XLA Ops:
  0.0 26.6 %shard_map.82 = f32[5,32,128]{2,1,0:T(8,128)S(1)} custom-call(f32[5,32,128]{2,1,0:T(8,128)} %bitcast.11, f32[5,5,32,128]{3,2,1,0:T(8,128)} %bitcast.9, f32[5,32,128]{2,1,0:T(8,128)} %bitcast.12, f32[5,6,5]{2,1,0:T(8,128)} %bitcast.13, f32[50,2,512]{2,1,0:T(2,128)} %bitcast.10, s32[2]{0:T(128)} %cutoffs_in.1, bf16[1024,128]{1,0:T(8,128)(2,1)} %constant.4.clone.const_in, ...), custom_call_target="tpu_custom_call" | custom-call | tf_op jit(solution)/shard_map/pallas_call | solution.py:523
  26.6 0.6 %copy.10 = f32[5,4,8,128]{3,2,1,0:T(8,128)} copy(f32[5,4,8,128]{3,2,1,0:T(8,128)S(1)} %bitcast.8) | data formatting | bytes 163840
